TPU v7x, 768 devices: a whole 4x8x12 slice. The times are simulated.
768 devices in a mesh: shore: 24 (over z_hi, x, core), cross: 32 (over z_lo, y).
Axes of the slice: x: 4, y: 8, z: 12 (z_hi: 3, z_lo: 4; z = z_hi * 4 + z_lo), core: 2. Of those that a mesh axis runs over, the one named last changes fastest.
Arguments:
- positions: float32 [2, 384, 256, 128], P(None, 'shore', 'cross'), may hold values from 0 to 1
- velocity: float32 [2, 384, 256, 128], P(None, 'shore', 'cross'), may hold values from -3 to 3
- density: float32 [384, 256, 128], P('shore', 'cross'), may hold values from 0.97 to 1.03
- particle_mass: float32 [384, 256, 128], P('shore', 'cross'), may hold values from 0.004 to 0.016
- cell_count: int32 [384, 256], P('shore', 'cross'), may hold values from 0 to 128
- wind_seed: int32 [384, 256, 128], P('shore', 'cross'), may hold values from 0 to 15
- wind_table: float32 [2, 16], replicated, may hold values from -4 to 4
- migrant_slot: int32 [24, 32, 4, 1792], P('shore', 'cross'), may hold values from 0 to 16383
- migrant_count: int32 [24, 32, 4], P('shore', 'cross'), may hold values from 896 to 1792, as said below
Outputs:
- state_next: float32 [7, 384, 256, 128], P(None, 'shore', 'cross')
- arrivals: float32 [24, 32, 4, 8, 1792], P('shore', 'cross')
Inputs may be any that keep to these rules, and one draw needn't show every extreme that they name: `migrant_slot`: a slot in one device's own blocks, numbered (block along * 8 + block across) * 128 + slot. `migrant_count`: on every device, at least one direction has exactly 1792 migrants.
All inputs are finite; a program needn't handle non-finite values.
Results may differ from a plain program's by a relative error of at most 0.0003.
Values sent between devices are 32-bit elements; how exact they have to be, the bound alone decides.
A program may use at most 32 MiB of HBM per device.

v0:
```python
import functools

import jax
import jax.numpy as jnp
from jax import lax
from jax.sharding import Mesh
from jax.sharding import PartitionSpec as P

CROSS = ("cross_0", "cross_1")
SHORE = ("shore_0", "shore_1", "shore_2")
SHORE_CROSS = ("shore_0", "shore_1", "shore_2", "cross_0", "cross_1")


sound_speed = 10.0
smooth = 0.5
viscous = 0.1
kernel_norm = 7.0 / (4.0 * 3.141592653589793 * smooth * smooth)
grad_coef = -5.0 * kernel_norm / (smooth * smooth)


def passed_along(array, axis, by):
    peers = lax.axis_size(axis)
    pairs = [(i, i + by) for i in range(peers) if 0 <= i + by < peers]
    return lax.ppermute(array, axis, pairs)


def padded(cells, sides, width):
    for axis, dim in sides:
        count = lax.axis_size(axis)
        ends = count - 1
        head = lax.slice_in_dim(cells, 0, width, axis=dim)
        tail = lax.slice_in_dim(cells, cells.shape[dim] - width, cells.shape[dim], axis=dim)
        cells = jnp.concatenate(
            [
                lax.ppermute(tail, axis, [(i, (i + 1) % count) for i in range(ends)]),
                cells,
                lax.ppermute(head, axis, [((i + 1) % count, i) for i in range(ends)]),
            ],
            axis=dim,
        )
    return cells


def one_axis_at_a_time(array, axes):
    return functools.reduce(lax.pmax, axes, array)


def pressure_ratio(density):
    cube = density * density * density
    seventh = cube * cube * density
    pressure = sound_speed * sound_speed / 7.0 * (seventh - 1.0)
    return pressure / (density * density)


def pack_fields(positions, velocity, density, particle_mass, live_slots):
    return jnp.stack(
        [
            positions[0],
            positions[1],
            velocity[0],
            velocity[1],
            density,
            particle_mass,
            live_slots,
            pressure_ratio(density),
        ]
    )


def tile_terms(own_cells, near_cells, step_x, step_y):
    offset_x = own_cells[0][:, :, None] - near_cells[0][:, None, :] - step_x
    offset_y = own_cells[1][:, :, None] - near_cells[1][:, None, :] - step_y
    dist_sq = offset_x * offset_x + offset_y * offset_y
    radius = jnp.sqrt(dist_sq) / smooth
    falloff = jnp.maximum(1.0 - 0.5 * radius, 0.0)
    gradient = grad_coef * falloff * falloff * falloff
    relative_u = own_cells[2][:, :, None] - near_cells[2][:, None, :]
    relative_v = own_cells[3][:, :, None] - near_cells[3][:, None, :]
    approach = relative_u * offset_x + relative_v * offset_y
    viscous_mu = smooth * jnp.minimum(approach, 0.0) / (dist_sq + 0.01 * smooth * smooth)
    mean_density = 0.5 * (own_cells[4][:, :, None] + near_cells[4][:, None, :])
    visc_term = -viscous * sound_speed * viscous_mu / mean_density
    weighted = (near_cells[5] * near_cells[6])[:, None, :] * gradient
    coupling = weighted * (own_cells[7][:, :, None] + near_cells[7][:, None, :] + visc_term)
    force_x = -jnp.sum(coupling * offset_x, axis=2)
    force_y = -jnp.sum(coupling * offset_y, axis=2)
    density_rate = jnp.sum(weighted * approach, axis=2)
    return jnp.stack([force_x, force_y, density_rate])


def tile_both(own_cells, near_cells, step_x, step_y):
    offset_x = own_cells[0][:, :, None] - near_cells[0][:, None, :] - step_x
    offset_y = own_cells[1][:, :, None] - near_cells[1][:, None, :] - step_y
    dist_sq = offset_x * offset_x + offset_y * offset_y
    radius = jnp.sqrt(dist_sq) / smooth
    falloff = jnp.maximum(1.0 - 0.5 * radius, 0.0)
    gradient = grad_coef * falloff * falloff * falloff
    relative_u = own_cells[2][:, :, None] - near_cells[2][:, None, :]
    relative_v = own_cells[3][:, :, None] - near_cells[3][:, None, :]
    approach = relative_u * offset_x + relative_v * offset_y
    viscous_mu = smooth * jnp.minimum(approach, 0.0) / (dist_sq + 0.01 * smooth * smooth)
    mean_density = 0.5 * (own_cells[4][:, :, None] + near_cells[4][:, None, :])
    visc_term = -viscous * sound_speed * viscous_mu / mean_density
    shared = gradient * (own_cells[7][:, :, None] + near_cells[7][:, None, :] + visc_term)
    shared_x = shared * offset_x
    shared_y = shared * offset_y
    rate_part = gradient * approach
    near_mass = (near_cells[5] * near_cells[6])[:, None, :]
    own_mass = (own_cells[5] * own_cells[6])[:, :, None]
    front = jnp.stack(
        [
            -jnp.sum(near_mass * shared_x, axis=2),
            -jnp.sum(near_mass * shared_y, axis=2),
            jnp.sum(near_mass * rate_part, axis=2),
        ]
    )
    behind = jnp.stack(
        [
            jnp.sum(own_mass * shared_x, axis=1),
            jnp.sum(own_mass * shared_y, axis=1),
            jnp.sum(own_mass * rate_part, axis=1),
        ]
    )
    return (front, behind)


def half_row(three_rows):
    own_cells = three_rows[:, 1, 1:-1]
    width = own_cells.shape[1]
    own_sum = tile_terms(own_cells, own_cells, 0.0, 0.0)
    front, behind = tile_both(own_cells, three_rows[:, 1, 2 : 2 + width], 0.0, 1.0)
    own_sum = own_sum + front
    row_here = jnp.pad(behind, ((0, 0), (2, 0), (0, 0)))
    row_next = jnp.zeros_like(row_here)
    for step_y in (-1, 0, 1):
        near_cells = three_rows[:, 2, 1 + step_y : 1 + step_y + width]
        front, behind = tile_both(own_cells, near_cells, 1.0, float(step_y))
        own_sum = own_sum + front
        row_next = row_next + jnp.pad(behind, ((0, 0), (1 + step_y, 1 - step_y), (0, 0)))
    row_here = row_here + jnp.pad(own_sum, ((0, 0), (1, 1), (0, 0)))
    return (row_here, row_next)


def across_return(block, offset):
    return passed_along(block, CROSS, offset)


def half_forces(extended):
    row_count = extended.shape[1] - 2
    col_count = extended.shape[2] - 2

    def one_row(row_index):
        return half_row(lax.dynamic_slice_in_dim(extended, row_index, 3, 1))

    here_rows, next_rows = lax.map(one_row, jnp.arange(row_count, dtype=jnp.int32))
    here_rows = jnp.transpose(here_rows, (1, 0, 2, 3))
    next_rows = jnp.transpose(next_rows, (1, 0, 2, 3))
    total = jnp.pad(here_rows, ((0, 0), (1, 1), (0, 0), (0, 0))) + jnp.pad(
        next_rows, ((0, 0), (2, 0), (0, 0), (0, 0))
    )
    arrived = passed_along(total[:, row_count + 1], SHORE, 1)
    total = total.at[:, 1].add(arrived)
    upper = across_return(total[:, 1 : row_count + 1, col_count + 1], 1)
    lower = across_return(total[:, 1 : row_count + 1, 0], -1)
    total = total.at[:, 1 : row_count + 1, 1].add(upper)
    total = total.at[:, 1 : row_count + 1, col_count].add(lower)
    return total[:, 1 : row_count + 1, 1 : col_count + 1]


def time_step(peak_acc, peak_speed):
    return 0.25 * smooth / (sound_speed + peak_speed + jnp.sqrt(smooth * peak_acc))


def pick_migrants(flattened, slot_list, live_count):
    width = slot_list.shape[1]
    picked = jnp.take(flattened, slot_list.reshape(-1), axis=1)
    picked = jnp.transpose(picked.reshape(flattened.shape[0], 4, width), (1, 0, 2))
    live_rows = (jnp.arange(width, dtype=jnp.int32)[None, :] < live_count[:, None]).astype(
        jnp.float32
    )
    return picked * live_rows[:, None, :]


def along_shore(block, offset):
    return passed_along(block, SHORE, offset)


def across_shore(block, offset):
    return passed_along(block, CROSS, offset)


def body(
    positions,
    velocity,
    density,
    particle_mass,
    cell_count,
    wind_seed,
    wind_table,
    migrant_slot,
    migrant_count,
):
    slot_total = positions.shape[3]
    slot_ids = jnp.arange(slot_total, dtype=jnp.int32)
    live_slots = (slot_ids[None, None, :] < cell_count[:, :, None]).astype(jnp.float32)
    fields = pack_fields(positions, velocity, density, particle_mass, live_slots)
    extended = padded(fields, ((SHORE, 1), (CROSS, 2)), 1)
    forces = half_forces(extended)
    level_ids = jnp.arange(wind_table.shape[1], dtype=jnp.int32)
    one_hot = (wind_seed[None] == level_ids[:, None, None, None]).astype(jnp.float32)
    windage = jnp.einsum("cl,lxyp->cxyp", wind_table, one_hot, precision=lax.Precision.HIGHEST)
    acceleration = (forces[:2] + windage) * live_slots[None]
    density_rate = forces[2] * live_slots
    local_acc = jnp.max(
        jnp.sqrt(acceleration[0] * acceleration[0] + acceleration[1] * acceleration[1])
    )
    local_speed = jnp.max(
        jnp.sqrt(velocity[0] * velocity[0] + velocity[1] * velocity[1]) * live_slots
    )
    peak_acc, peak_speed = (
        one_axis_at_a_time(local_acc, SHORE_CROSS),
        one_axis_at_a_time(local_speed, SHORE_CROSS),
    )
    delta_t = time_step(peak_acc, peak_speed)
    new_velocity = (velocity + delta_t * acceleration) * live_slots[None]
    new_position = (positions + delta_t * new_velocity) * live_slots[None]
    new_density = (density + delta_t * density_rate) * live_slots
    state_next = jnp.concatenate([new_position, new_velocity, new_density[None], acceleration])
    carried = jnp.concatenate(
        [
            new_position,
            new_velocity,
            new_density[None],
            (particle_mass * live_slots)[None],
            acceleration,
        ]
    )
    flattened = carried.reshape(carried.shape[0], -1)
    leaving = pick_migrants(flattened, migrant_slot[0, 0], migrant_count[0, 0])
    eastward = along_shore(leaving[0], 1)
    westward = along_shore(leaving[1], -1)
    northward = across_shore(leaving[2], 1)
    southward = across_shore(leaving[3], -1)
    arrivals = jnp.stack([eastward, westward, northward, southward])[None, None]
    return (state_next, arrivals)


def solution(mesh):
    split = Mesh(
        mesh.devices.reshape(3, 4, 2, 4, 8), ("shore_0", "shore_1", "shore_2", "cross_0", "cross_1")
    )
    placed = (
        P(None, SHORE, CROSS, None),
        P(None, SHORE, CROSS, None),
        P(SHORE, CROSS, None),
        P(SHORE, CROSS, None),
        P(SHORE, CROSS),
        P(SHORE, CROSS, None),
        P(),
        P(SHORE, CROSS, None, None),
        P(SHORE, CROSS, None),
    )
    return jax.shard_map(
        body,
        mesh=split,
        in_specs=placed,
        out_specs=(P(None, SHORE, CROSS, None), P(SHORE, CROSS, None, None, None)),
        check_vma=False,
    )
```

profile of v0, /device:TPU:1, one launch (start us, length us, event | category | flops | bytes accessed | tf_op | source)
XLA Modules:
  0.0 336.2 jit_solution(8315281884286589959)
XLA Ops:
  6.0 4.5 %collective-permute-start = (f32[8,1,8,128]{3,2,1,0:T(8,128)S(1)}, f32[8,1,8,128]{3,2,1,0:T(8,128)S(1)}, u32[]{:S(2)}, u32[]{:S(2)}) collective-permute-start(f32[8,1,8,128]{3,2,1,0:T(8,128)S(1)} %get-tuple-element.244), channel_id=1, source_target_pairs={{0,32},{32,64},{64,96},{96,128},{128,160},{160,192},{192,224},{224... | collective-permute-start | bytes 98312 | tf_op jit(solution)/shard_map/ppermute | solution.py:35
  10.5 9.2 %collective-permute-start.1 = (f32[8,1,8,128]{3,2,1,0:T(8,128)S(1)}, f32[8,1,8,128]{3,2,1,0:T(8,128)S(1)}, u32[]{:S(2)}, u32[]{:S(2)}) collective-permute-start(f32[8,1,8,128]{3,2,1,0:T(8,128)S(1)} %get-tuple-element.245), channel_id=1, source_target_pairs={{32,0},{64,32},{96,64},{128,96},{160,128},{192,160},{224,192},{256... | collective-permute-start | bytes 98312 | tf_op jit(solution)/shard_map/ppermute | solution.py:37
  24.5 3.8 %collective-permute-done.3 = f32[8,18,1,128]{3,2,1,0:T(1,128)S(1)} collective-permute-done((f32[8,18,1,128]{3,2,1,0:T(1,128)S(1)}, f32[8,18,1,128]{3,2,1,0:T(1,128)S(1)}, u32[]{:S(2)}, u32[]{:S(2)}) %collective-permute-start.3) | collective-permute-done | bytes 73760 | tf_op jit(solution)/shard_map/ppermute | solution.py:37
  28.6 170.1 %while.18 = (s32[]{:T(128)}, f32[16,3,10,128]{3,1,2,0:T(4,128)S(1)}, f32[16,3,10,128]{3,1,2,0:T(4,128)S(1)}, s32[16]{0:T(128)S(1)}, f32[8,18,10,128]{3,2,1,0:T(8...) while((s32[]{:T(128)}, ...), condition=%wide.region_34.35_spmd, body=%wide.region_6.34_spmd.sunk | while | flops 26749708 | bytes 985423 | solution.py:155
  31.3 2.6 multiply_reduce_fusion.32
  33.9 1.7 multiply_reduce_fusion.31
  37.4 1.7 multiply_reduce_fusion.29
  41.9 2.6 multiply_reduce_fusion.32
  44.5 1.7 multiply_reduce_fusion.31
  48.0 1.7 multiply_reduce_fusion.29
  52.5 2.6 multiply_reduce_fusion.32
  55.1 1.7 multiply_reduce_fusion.31
  58.6 1.7 multiply_reduce_fusion.29
  63.2 2.6 multiply_reduce_fusion.32
  65.8 1.7 multiply_reduce_fusion.31
  69.2 1.7 multiply_reduce_fusion.29
  73.8 2.6 multiply_reduce_fusion.32
  76.4 1.7 multiply_reduce_fusion.31
  79.9 1.7 multiply_reduce_fusion.29
  84.4 2.6 multiply_reduce_fusion.32
  87.0 1.7 multiply_reduce_fusion.31
  90.5 1.7 multiply_reduce_fusion.29
  95.0 2.6 multiply_reduce_fusion.32
  105.7 2.6 multiply_reduce_fusion.32
  116.3 2.6 multiply_reduce_fusion.32
  126.9 2.6 multiply_reduce_fusion.32
  137.6 2.6 multiply_reduce_fusion.32
  148.2 2.6 multiply_reduce_fusion.32
  154.3 1.7 multiply_reduce_fusion.29
  158.8 2.6 multiply_reduce_fusion.32
  169.5 2.6 multiply_reduce_fusion.32
  172.1 1.7 multiply_reduce_fusion.31
  180.1 2.6 multiply_reduce_fusion.32
  190.7 2.6 multiply_reduce_fusion.32
  198.7 2.1 collective-permute-start.4
  205.7 2.9 collective-permute-done.6
  209.4 22.2 %all-reduce.10 = (f32[]{:T(128)}, f32[]{:T(128)}) all-reduce(f32[]{:T(128)} %fusion.93, f32[]{:T(128)} %fusion.92), channel_id=1, replica_groups=mesh['shore_0'=3,'shore_1'=4,'shore_2'=2,'cross_0'=4,'cross_1'=8] {'shor..., use_global_device_ids=true, to_apply=%region_1.0 | all-reduce | flops 2 | bytes 16 | tf_op jit(solution)/shard_map/pmax | solution.py:45
  231.6 11.8 %all-reduce.9 = (f32[]{:T(128)}, f32[]{:T(128)}) all-reduce(f32[]{:T(128)} %get-tuple-element.197, f32[]{:T(128)} %get-tuple-element.198), channel_id=1, replica_groups=mesh['shore_0'=3,'shore_1'=4,'shore_2'=2,'cross_0'=4,'cross_1'=8] {'shor..., use_global_device_ids=true, to_apply=%region_2.0 | all-reduce | flops 2 | bytes 16 | tf_op jit(solution)/shard_map/pmax | solution.py:45
  243.4 10.1 %all-reduce.11 = (f32[]{:T(128)}, f32[]{:T(128)}) all-reduce(f32[]{:T(128)} %get-tuple-element.195, f32[]{:T(128)} %get-tuple-element.196), channel_id=1, replica_groups=mesh['shore_0'=3,'shore_1'=4,'shore_2'=2,'cross_0'=4,'cross_1'=8] {'shor..., use_global_device_ids=true, to_apply=%region_3.0 | all-reduce | flops 2 | bytes 16 | tf_op jit(solution)/shard_map/pmax | solution.py:45
  253.6 11.1 %all-reduce.8 = (f32[]{:T(128)}, f32[]{:T(128)}) all-reduce(f32[]{:T(128)} %get-tuple-element.199, f32[]{:T(128)} %get-tuple-element.200), channel_id=1, replica_groups=mesh['shore_0'=3,'shore_1'=4,'shore_2'=2,'cross_0'=4,'cross_1'=8] {'cros..., use_global_device_ids=true, to_apply=%region_4.0 | all-reduce | flops 2 | bytes 16 | tf_op jit(solution)/shard_map/pmax | solution.py:45
  264.7 14.2 %all-reduce.7 = (f32[]{:T(128)}, f32[]{:T(128)}) all-reduce(f32[]{:T(128)} %get-tuple-element.193, f32[]{:T(128)} %get-tuple-element.194), channel_id=1, replica_groups=mesh['shore_0'=3,'shore_1'=4,'shore_2'=2,'cross_0'=4,'cross_1'=8] {'cros..., use_global_device_ids=true, to_apply=%region_5.0 | all-reduce | flops 2 | bytes 16 | tf_op jit(solution)/shard_map/pmax | solution.py:45
  281.3 5.3 %copy.81 = f32[8,16384]{0,1:T(8,128)} copy(f32[8,16384]{1,0:T(8,128)S(1)} %concatenate.38) | data formatting | bytes 1048576 | tf_op jit(solution)/shard_map/concatenate | solution.py:229
  286.5 27.5 %gather_fusion = f32[7168,8]{1,0:T(8,128)} fusion(f32[8,16384]{0,1:T(8,128)} %copy.81, s32[7168]{0:T(1024)S(1)} %broadcast_clamp_fusion), kind=kCustom, calls=%fused_computation | custom fusion | bytes 487424 | tf_op jit(solution)/shard_map/jit(_take)/gather | solution.py:176
  314.1 2.5 copy.82
  316.7 9.5 %collective-permute-start.7 = (f32[8,1792]{1,0:T(8,128)S(1)}, f32[8,1792]{1,0:T(8,128)S(1)}, u32[]{:S(2)}, u32[]{:S(2)}) collective-permute-start(f32[8,1792]{1,0:T(8,128)S(1)} %get-tuple-element.248), channel_id=1, source_target_pairs={{0,32},{32,64},{64,96},{96,128},{128,160},{160,192},{192,224},{224... | collective-permute-start | bytes 172040 | tf_op jit(solution)/shard_map/ppermute | solution.py:24
  326.2 1.9 collective-permute-start.8
  328.1 2.4 collective-permute-start.9
  332.7 2.8 collective-permute-done.10
  (362 shorter events, 91.5 us)
Async XLA Ops:
  0.6 20.0 %copy-start = (f32[2,16]{1,0:T(2,128)S(1)}, f32[2,16]{1,0:T(2,128)}, u32[]{:S(2)}) copy-start(f32[2,16]{1,0:T(2,128)} %param.23) | copy-start | bytes 388
  0.6 19.8 %copy-start.5 = (s32[1,1,4,1792]{3,2,1,0:T(4,128)S(1)}, s32[1,1,4,1792]{3,2,1,0:T(4,128)}, u32[]{:S(2)}) copy-start(s32[1,1,4,1792]{3,2,1,0:T(4,128)} %param.24) | copy-start | bytes 86020
  0.7 19.8 %copy-start.6 = (s32[1,1,4]{2,1,0:T(1,128)S(1)}, s32[1,1,4]{2,1,0:T(1,128)}, u32[]{:S(2)}) copy-start(s32[1,1,4]{2,1,0:T(1,128)} %param.25) | copy-start | bytes 52
  0.7 19.9 %copy-start.7 = (s32[16,8,128]{2,1,0:T(8,128)S(1)}, s32[16,8,128]{2,1,0:T(8,128)}, u32[]{:S(2)}) copy-start(s32[16,8,128]{2,1,0:T(8,128)} %param.22) | copy-start | bytes 196612
  6.0 15.0 %collective-permute-start = (f32[8,1,8,128]{3,2,1,0:T(8,128)S(1)}, f32[8,1,8,128]{3,2,1,0:T(8,128)S(1)}, u32[]{:S(2)}, u32[]{:S(2)}) collective-permute-start(f32[8,1,8,128]{3,2,1,0:T(8,128)S(1)} %get-tuple-element.244), channel_id=1, source_target_pairs={{0,32},{32,64},{64,96},{96,128},{128,160},{160,192},{192,224},{224... | collective-permute-start | bytes 98312 | tf_op jit(solution)/shard_map/ppermute | solution.py:35
  10.5 10.5 %collective-permute-start.1 = (f32[8,1,8,128]{3,2,1,0:T(8,128)S(1)}, f32[8,1,8,128]{3,2,1,0:T(8,128)S(1)}, u32[]{:S(2)}, u32[]{:S(2)}) collective-permute-start(f32[8,1,8,128]{3,2,1,0:T(8,128)S(1)} %get-tuple-element.245), channel_id=1, source_target_pairs={{32,0},{64,32},{96,64},{128,96},{160,128},{192,160},{224,192},{256... | collective-permute-start | bytes 98312 | tf_op jit(solution)/shard_map/ppermute | solution.py:37
  21.1 3.4 %collective-permute-start.2 = (f32[8,18,1,128]{3,2,1,0:T(1,128)S(1)}, f32[8,18,1,128]{3,2,1,0:T(1,128)S(1)}, u32[]{:S(2)}, u32[]{:S(2)}) collective-permute-start(f32[8,18,1,128]{3,2,1,0:T(1,128)S(1)} %get-tuple-element.242), channel_id=1, source_target_pairs={{0,1},{1,2},{2,3},{3,4},{4,5},{5,6},{6,7},{7,8},{8,9},{9,10},{10,1... | collective-permute-start | bytes 221192 | tf_op jit(solution)/shard_map/ppermute | solution.py:35
  22.4 5.9 %collective-permute-start.3 = (f32[8,18,1,128]{3,2,1,0:T(1,128)S(1)}, f32[8,18,1,128]{3,2,1,0:T(1,128)S(1)}, u32[]{:S(2)}, u32[]{:S(2)}) collective-permute-start(f32[8,18,1,128]{3,2,1,0:T(1,128)S(1)} %get-tuple-element.243), channel_id=1, source_target_pairs={{1,0},{2,1},{3,2},{4,3},{5,4},{6,5},{7,6},{8,7},{9,8},{10,9},{11,1... | collective-permute-start | bytes 221192 | tf_op jit(solution)/shard_map/ppermute | solution.py:37
  198.7 4.7 %copy-start.1 = (f32[2,16,8,128]{3,2,1,0:T(8,128)S(1)}, f32[2,16,8,128]{3,2,1,0:T(8,128)}, u32[]{:S(2)}) copy-start(f32[2,16,8,128]{3,2,1,0:T(8,128)} %param.18) | copy-start | bytes 393220
  198.7 3.2 collective-permute-start.4
  200.9 79.3 %copy-start.3 = (f32[2,16,8,128]{3,2,1,0:T(8,128)S(1)}, f32[2,16,8,128]{3,2,1,0:T(8,128)}, u32[]{:S(2)}) copy-start(f32[2,16,8,128]{3,2,1,0:T(8,128)} %param.17) | copy-start | bytes 393220
  202.1 3.3 collective-permute-start.5
  204.1 4.6 %collective-permute-start.6 = (f32[3,16,128]{2,1,0:T(8,128)S(1)}, f32[3,16,128]{2,1,0:T(8,128)S(1)}, u32[]{:S(2)}, u32[]{:S(2)}) collective-permute-start(f32[3,16,128]{2,1,0:T(8,128)S(1)} %get-tuple-element.246), channel_id=1, source_target_pairs={{1,0},{2,1},{3,2},{4,3},{5,4},{6,5},{7,6},{8,7},{9,8},{10,9},{11,1... | collective-permute-start | bytes 73736 | tf_op jit(solution)/shard_map/ppermute | solution.py:24
  205.6 74.6 %copy-start.2 = (f32[16,8,128]{2,1,0:T(8,128)S(1)}, f32[16,8,128]{2,1,0:T(8,128)}, u32[]{:S(2)}) copy-start(f32[16,8,128]{2,1,0:T(8,128)} %param.19) | copy-start | bytes 196612
  205.6 74.6 %copy-start.4 = (f32[16,8,128]{2,1,0:T(8,128)S(1)}, f32[16,8,128]{2,1,0:T(8,128)}, u32[]{:S(2)}) copy-start(f32[16,8,128]{2,1,0:T(8,128)} %param.20) | copy-start | bytes 196612
  316.7 16.0 %collective-permute-start.7 = (f32[8,1792]{1,0:T(8,128)S(1)}, f32[8,1792]{1,0:T(8,128)S(1)}, u32[]{:S(2)}, u32[]{:S(2)}) collective-permute-start(f32[8,1792]{1,0:T(8,128)S(1)} %get-tuple-element.248), channel_id=1, source_target_pairs={{0,32},{32,64},{64,96},{96,128},{128,160},{160,192},{192,224},{224... | collective-permute-start | bytes 172040 | tf_op jit(solution)/shard_map/ppermute | solution.py:24
  326.2 6.5 %collective-permute-start.8 = (f32[8,1792]{1,0:T(8,128)S(1)}, f32[8,1792]{1,0:T(8,128)S(1)}, u32[]{:S(2)}, u32[]{:S(2)}) collective-permute-start(f32[8,1792]{1,0:T(8,128)S(1)} %get-tuple-element.251), channel_id=1, source_target_pairs={{32,0},{64,32},{96,64},{128,96},{160,128},{192,160},{224,192},{256... | collective-permute-start | bytes 172040 | tf_op jit(solution)/shard_map/ppermute | solution.py:24
  328.1 4.5 %collective-permute-start.9 = (f32[8,1792]{1,0:T(8,128)S(1)}, f32[8,1792]{1,0:T(8,128)S(1)}, u32[]{:S(2)}, u32[]{:S(2)}) collective-permute-start(f32[8,1792]{1,0:T(8,128)S(1)} %get-tuple-element.250), channel_id=1, source_target_pairs={{0,1},{1,2},{2,3},{3,4},{4,5},{5,6},{6,7},{7,8},{8,9},{9,10},{10,1... | collective-permute-start | bytes 172040 | tf_op jit(solution)/shard_map/ppermute | solution.py:24
  330.5 4.9 %collective-permute-start.10 = (f32[8,1792]{1,0:T(8,128)S(1)}, f32[8,1792]{1,0:T(8,128)S(1)}, u32[]{:S(2)}, u32[]{:S(2)}) collective-permute-start(f32[8,1792]{1,0:T(8,128)S(1)} %get-tuple-element.249), channel_id=1, source_target_pairs={{1,0},{2,1},{3,2},{4,3},{5,4},{6,5},{7,6},{8,7},{9,8},{10,9},{11,1... | collective-permute-start | bytes 172040 | tf_op jit(solution)/shard_map/ppermute | solution.py:24
where the time goes:
time: 341 us; the launch traced here: 336 us
  other arithmetic  131 us (38%)
  blocking collectives  69.4 us (20%)
  local copies, waits for them, and re-layouts  51.9 us (15%)
  starting transfers between devices  36 us (11%)
  loops' own time  33.5 us (10%)
  waiting for transfers between devices  11.2 us (3%)
    reduce_sum x48, other arithmetic, tile_both(): jnp.sum(own_mass * shared_x, axis=1)  82.4 us
    pmax x5, blocking collectives, one_axis_at_a_time(): return functools.reduce(lax.pmax, axes, array)  69.4 us
    reduce_sum x16, other arithmetic, tile_both(): jnp.sum(near_mass * shared_x, axis=2)  40.8 us
    another operation x1, loops' own time, half_forces(): lax.map(one_row, jnp.arange(row_count, dtype=jnp.int32))  33.5 us
    gather x2, local copies, waits for them, and re-layouts, pick_migrants(): picked = jnp.take(flattened, slot_list.reshape(-1), axis=1)  30.1 us
    ppermute x7, starting transfers between devices, passed_along(): return lax.ppermute(array, axis, pairs)  19.7 us
    ppermute x2, starting transfers between devices, padded(): lax.ppermute(head, axis, [((i + 1) % count, i) for i in range(ends)])  10.5 us
    dynamic_slice x16, local copies, waits for them, and re-layouts, half_forces(): lax.map(one_row, jnp.arange(row_count, dtype=jnp.int32))  9.38 us
  transfers between devices with their start and end apart: 11, of which 5 were waited for; matrix products, arithmetic and copies ran while one was open for 1% of the time, Pallas kernels for 0%

commit v1 on v0

v1 whole, which is shorter than its diff:
```python
import functools

import jax
import jax.numpy as jnp
from jax import lax
from jax.experimental import pallas as pl
from jax.experimental.pallas import tpu as pltpu
from jax.sharding import PartitionSpec as P

MESH = pl.DeviceIdType.MESH
SUB, LANES = 8, 128
GROUP = 2
FIELDS = 7
TILE = 256
TINY = 1e-30

sound_speed = 10.0
smooth = 0.5
viscous = 0.1
kernel_norm = 7.0 / (4.0 * 3.141592653589793 * smooth * smooth)
grad_coef = -5.0 * kernel_norm / (smooth * smooth)


def pressure_ratio(density):
    cube = density * density * density
    seventh = cube * cube * density
    pressure = sound_speed * sound_speed / 7.0 * (seventh - 1.0)
    return pressure / (density * density)


def padded(cells, sides):
    for axis, dim in sides:
        ends = lax.axis_size(axis) - 1
        head = lax.slice_in_dim(cells, 0, 1, axis=dim)
        tail = lax.slice_in_dim(cells, cells.shape[dim] - 1, cells.shape[dim], axis=dim)
        cells = jnp.concatenate(
            [
                lax.ppermute(tail, axis, [(i, i + 1) for i in range(ends)]),
                cells,
                lax.ppermute(head, axis, [(i + 1, i) for i in range(ends)]),
            ],
            axis=dim,
        )
    return cells


def halves(exact, parts):
    got = []
    for _ in range(parts):
        got.append(exact.astype(jnp.bfloat16))
        exact = exact - got[-1].astype(jnp.float32)
    return got


def force_kernel(
    counts_ref, table_ref, cells_ref, pick_ref, seed_ref, live_ref, base_ref, out_ref, peak_ref, placed, wide, sums
):
    height, width = cells_ref.shape[:2]
    rows, cols = height - 2, width - 2
    field = lax.broadcasted_iota(jnp.int32, (SUB, LANES), 0)

    @pl.loop(0, height)
    def _(row):
        for col in range(width):
            shift = jnp.where(field == 0, row.astype(jnp.float32), jnp.where(field == 1, float(col), 0.0))
            placed[row, col] = cells_ref[row, col] + shift

    @pl.loop(0, rows)
    def _(row):
        for col in range(cols):
            for c in range(3):
                sums[row, col, c] = jnp.zeros((SUB, LANES), jnp.float32)

    def widen(row):
        for col in range(width):
            split = jnp.concatenate([x.astype(jnp.float32) for x in halves(placed[row, col], 3)], axis=0)
            wide[col] = lax.dot_general(
                jnp.transpose(split).astype(jnp.bfloat16),
                pick_ref[...],
                (((1,), (0,)), ((), ())),
                preferred_element_type=jnp.float32,
            )

    def one_cell(row, col, row_steps, col_steps):
        count = lax.div(counts_ref[row, col] + (SUB * GROUP - 1), SUB * GROUP)

        @pl.loop(0, count)
        def _(part):
            near = []
            for g in range(GROUP):
                at = pl.ds(pl.multiple_of((part * GROUP + g) * SUB, SUB), SUB)
                near.append(tuple(wide[col, at, f * LANES : (f + 1) * LANES] for f in range(FIELDS)))
            for dr in row_steps:
                for dc in col_steps:
                    xi, yi, ui, vi, di, pi = (
                        jnp.broadcast_to(placed[row + dr, col + dc, f : f + 1, :], (SUB, LANES)) for f in range(6)
                    )
                    fx = fy = rate = None
                    for g in range(GROUP):
                        xj, yj, uj, vj, dj, pj, mj = near[g]
                        ox = xi - xj
                        oy = yi - yj
                        d2 = ox * ox + oy * oy
                        r = d2 * lax.rsqrt(jnp.maximum(d2, TINY))
                        f = jnp.maximum(1.0 - r, 0.0)
                        w = mj * (f * f * f)
                        a = (ui - uj) * ox + (vi - vj) * oy
                        q = (d2 + 0.01 * smooth * smooth) * (di + dj)
                        c = w * ((pi + pj) - jnp.minimum(a, 0.0) * pl.reciprocal(q))
                        fx = c * ox if g == 0 else fx + c * ox
                        fy = c * oy if g == 0 else fy + c * oy
                        rate = w * a if g == 0 else rate + w * a
                    own = (row + dr - 1, col + dc - 1)
                    sums[own[0], own[1], 0] += fx
                    sums[own[0], own[1], 1] += fy
                    sums[own[0], own[1], 2] += rate

    def one_row(row, row_steps):
        widen(row)
        one_cell(row, 0, row_steps, (1,))
        one_cell(row, 1, row_steps, (0, 1))

        @pl.loop(2, width - 2)
        def _(col):
            one_cell(row, col, row_steps, (-1, 0, 1))

        one_cell(row, width - 2, row_steps, (-1, 0))
        one_cell(row, width - 1, row_steps, (-1,))

    one_row(0, (1,))
    one_row(1, (0, 1))

    @pl.loop(2, height - 2)
    def _(row):
        one_row(row, (-1, 0, 1))

    one_row(height - 2, (-1, 0))
    one_row(height - 1, (-1,))

    def finish(row, peaks):
        live = live_ref[row]
        seed = seed_ref[row]
        got = []
        for c in range(3):
            got.append(
                jnp.concatenate(
                    [jnp.sum(sums[row, col, c], axis=0, keepdims=True) for col in range(cols)], axis=0
                )
            )
        acc = []
        for c in range(2):
            wind = jnp.full(seed.shape, table_ref[c, 0], jnp.float32)
            for level in range(1, table_ref.shape[1]):
                wind = jnp.where(seed == level, table_ref[c, level], wind)
            acc.append((wind - got[c]) * live)
            out_ref[c, row] = acc[c]
        out_ref[2, row] = got[2] * live
        vx, vy = base_ref[2, row], base_ref[3, row]
        return (
            jnp.maximum(peaks[0], acc[0] * acc[0] + acc[1] * acc[1]),
            jnp.maximum(peaks[1], vx * vx + vy * vy),
        )

    zero = jnp.zeros((cols, LANES), jnp.float32)
    peaks = lax.fori_loop(0, rows, finish, (zero, zero))
    peak_ref[...] = jnp.where(field < 4, jnp.max(peaks[0]), jnp.max(peaks[1]))


def all_forces(counts, table, cells, seed, live, base):
    height, width = cells.shape[:2]
    rows, cols = height - 2, width - 2
    which = lax.broadcasted_iota(jnp.int32, (24, FIELDS * LANES), 0) % 8
    pick = (which == lax.broadcasted_iota(jnp.int32, (24, FIELDS * LANES), 1) // LANES).astype(jnp.bfloat16)
    return pl.pallas_call(
        force_kernel,
        out_shape=(
            jax.ShapeDtypeStruct((3, rows, cols, LANES), jnp.float32),
            jax.ShapeDtypeStruct((SUB, LANES), jnp.float32),
        ),
        in_specs=[pl.BlockSpec(memory_space=pltpu.SMEM)] * 2 + [pl.BlockSpec(memory_space=pltpu.VMEM)] * 5,
        out_specs=(pl.BlockSpec(memory_space=pltpu.VMEM),) * 2,
        scratch_shapes=[
            pltpu.VMEM((height, width, SUB, LANES), jnp.float32),
            pltpu.VMEM((width, LANES, FIELDS * LANES), jnp.float32),
            pltpu.VMEM((rows, cols, 3, SUB, LANES), jnp.float32),
        ],
        compiler_params=pltpu.CompilerParams(vmem_limit_bytes=32 << 20),
    )(counts, table, cells, pick, seed, live, base)


def exchange_kernel(
    groups, counts_ref, slots_ref, base_ref, moved_ref, peak_ref, got_ref, top_ref,
    split, leaving, held, heap_a, heap_b, heap_c, send_a, recv_a, send_b, recv_b, send_c, recv_c, send_m, recv_m,
):
    inner, outer, near, far = groups
    shore, cross = lax.axis_index("shore"), lax.axis_index("cross")
    shores, crosses = inner * outer, near * far
    s_out, s_in = lax.div(shore, inner), lax.rem(shore, inner)
    c_out, c_in = lax.div(cross, near), lax.rem(cross, near)

    along = [
        (s_out * inner + lax.rem(s_in + o, inner), cross) for o in range(1, inner)
    ]
    across = [(shore, c_out * near + lax.rem(c_in + o, near)) for o in range(1, near)]
    depth = []
    for o in range(1, outer * far):
        spot = lax.rem(s_out * far + c_out + o, outer * far)
        depth.append((lax.div(spot, far) * inner + s_in, lax.rem(spot, far) * near + c_in))
    ends = [
        (shore < shores - 1, shore > 0, (shore + 1, cross)),
        (shore > 0, shore < shores - 1, (shore - 1, cross)),
        (cross < crosses - 1, cross > 0, (shore, cross + 1)),
        (cross > 0, cross < crosses - 1, (shore, cross - 1)),
    ]

    barrier = pltpu.get_barrier_semaphore()
    beside = [
        (lax.rem(shore + 1, shores), cross),
        (lax.rem(shore + shores - 1, shores), cross),
        (shore, lax.rem(cross + 1, crosses)),
        (shore, lax.rem(cross + crosses - 1, crosses)),
    ]
    greeted = along + across + depth + beside
    for peer in greeted:
        pl.semaphore_signal(barrier, inc=1, device_id=peer, device_id_type=MESH)

    kinds = base_ref.shape[0] + moved_ref.shape[0]
    cells = base_ref.shape[1] * base_ref.shape[2]
    for f in range(kinds):
        source = base_ref[f] if f < base_ref.shape[0] else moved_ref[f - base_ref.shape[0]]
        high, low = halves(source.reshape(cells, LANES), 2)
        split[f * cells : (f + 1) * cells, 0:LANES] = high
        split[f * cells : (f + 1) * cells, LANES : 2 * LANES] = low

    width = slots_ref.shape[1]
    rank = lax.broadcasted_iota(jnp.int32, (LANES, TILE), 0)
    for d in range(4):

        @pl.loop(0, width // TILE)
        def _(t):
            at = pl.ds(pl.multiple_of(t * TILE, TILE), TILE)
            slot = slots_ref[d : d + 1, at]
            lane = jnp.where(rank == (slot & (LANES - 1)), 1.0, 0.0)
            lanes = jnp.concatenate([lane, lane], axis=0).astype(jnp.bfloat16)
            order = lax.broadcasted_iota(jnp.int32, (1, TILE), 1) + t * TILE
            cell = jnp.where(order < counts_ref[d], lax.shift_right_logical(slot, 7), -1)
            keep = rank == cell
            for f in range(kinds):
                found = jnp.dot(
                    split[f * cells : (f + 1) * cells, :], lanes, preferred_element_type=jnp.float32
                )
                leaving[d, f : f + 1, at] = jnp.sum(jnp.where(keep, found, 0.0), axis=0, keepdims=True)

    pl.semaphore_wait(barrier, len(greeted))

    def migrants(d):
        return pltpu.make_async_remote_copy(
            src_ref=leaving.at[d],
            dst_ref=got_ref.at[d],
            send_sem=send_m.at[d],
            recv_sem=recv_m.at[d],
            device_id=ends[d][2],
            device_id_type=MESH,
        )

    held[0] = peak_ref[...]
    stages = ((along, heap_a, send_a, recv_a), (across, heap_b, send_b, recv_b), (depth, heap_c, send_c, recv_c))
    for step, (peers, heap, send, recv) in enumerate(stages):
        copies = [
            pltpu.make_async_remote_copy(
                src_ref=held.at[step],
                dst_ref=heap.at[o],
                send_sem=send.at[o],
                recv_sem=recv.at[o],
                device_id=peer,
                device_id_type=MESH,
            )
            for o, peer in enumerate(peers)
        ]
        for copy in copies:
            copy.start()
        if step == 0:
            for d in range(4):

                @pl.when(ends[d][0])
                def _():
                    migrants(d).start()

        top = held[step]
        for o, copy in enumerate(copies):
            copy.wait()
            top = jnp.maximum(top, heap[o])
        held[step + 1] = top
    top_ref[...] = held[len(stages)]

    for d in range(4):

        @pl.when(ends[d][0])
        def _():
            migrants(d).wait_send()

        @pl.when(ends[d][1])
        def _():
            migrants(d).wait_recv()

        @pl.when(jnp.logical_not(ends[d][1]))
        def _():
            got_ref[d] = jnp.zeros(got_ref.shape[1:], jnp.float32)


def exchange(groups, counts, slots, base, moved, peak):
    inner, outer, near, far = groups
    kinds = base.shape[0] + moved.shape[0]
    cells = base.shape[1] * base.shape[2]
    width = slots.shape[1]
    dma = pltpu.SemaphoreType.DMA
    sems = []
    for peers in (inner - 1, near - 1, outer * far - 1, 4):
        sems += [dma((peers,)), dma((peers,))]
    return pl.pallas_call(
        functools.partial(exchange_kernel, groups),
        out_shape=(
            jax.ShapeDtypeStruct((4, kinds, width), jnp.float32),
            jax.ShapeDtypeStruct((SUB, LANES), jnp.float32),
        ),
        in_specs=[pl.BlockSpec(memory_space=pltpu.SMEM)] + [pl.BlockSpec(memory_space=pltpu.VMEM)] * 4,
        out_specs=(pl.BlockSpec(memory_space=pltpu.VMEM),) * 2,
        scratch_shapes=[
            pltpu.VMEM((kinds * cells, 2 * LANES), jnp.bfloat16),
            pltpu.VMEM((4, kinds, width), jnp.float32),
            pltpu.VMEM((4, SUB, LANES), jnp.float32),
            pltpu.VMEM((inner - 1, SUB, LANES), jnp.float32),
            pltpu.VMEM((near - 1, SUB, LANES), jnp.float32),
            pltpu.VMEM((outer * far - 1, SUB, LANES), jnp.float32),
        ]
        + sems,
        compiler_params=pltpu.CompilerParams(collective_id=0, has_side_effects=True),
    )(counts, slots, base, moved, peak)


def advance_kernel(top_ref, base_ref, moved_ref, got_ref, state_ref, arrivals_ref):
    peak_acc = jnp.sqrt(jnp.max(top_ref[0:4], axis=(0, 1), keepdims=True))
    peak_speed = jnp.sqrt(jnp.max(top_ref[4:8], axis=(0, 1), keepdims=True))
    step = 0.25 * smooth / (sound_speed + peak_speed + jnp.sqrt(smooth * peak_acc))
    for c in range(2):
        speed = base_ref[2 + c] + step * moved_ref[c]
        state_ref[2 + c] = speed
        state_ref[c] = base_ref[c] + step * speed
        state_ref[5 + c] = moved_ref[c]
    state_ref[4] = base_ref[4] + step * moved_ref[2]
    for d in range(4):
        for c in range(2):
            push = got_ref[d, 6 + c : 7 + c]
            speed = got_ref[d, 2 + c : 3 + c] + step * push
            arrivals_ref[0, 0, d, 2 + c : 3 + c] = speed
            arrivals_ref[0, 0, d, c : c + 1] = got_ref[d, c : c + 1] + step * speed
            arrivals_ref[0, 0, d, 6 + c : 7 + c] = push
        arrivals_ref[0, 0, d, 4:5] = got_ref[d, 4:5] + step * got_ref[d, 8:9]
        arrivals_ref[0, 0, d, 5:6] = got_ref[d, 5:6]


def advance(top, base, moved, got):
    return pl.pallas_call(
        advance_kernel,
        out_shape=(
            jax.ShapeDtypeStruct((7,) + base.shape[1:], jnp.float32),
            jax.ShapeDtypeStruct((1, 1, 4, 8, got.shape[2]), jnp.float32),
        ),
        in_specs=[pl.BlockSpec(memory_space=pltpu.VMEM)] * 4,
        out_specs=(pl.BlockSpec(memory_space=pltpu.VMEM),) * 2,
    )(top, base, moved, got)


def body(
    groups, positions, velocity, density, particle_mass, cell_count, wind_seed, wind_table, migrant_slot, migrant_count
):
    slot_ids = jnp.arange(positions.shape[3], dtype=jnp.int32)
    live = (slot_ids[None, None, :] < cell_count[:, :, None]).astype(jnp.float32)
    base = jnp.concatenate(
        [positions * live, velocity * live, (density * live)[None], (particle_mass * live)[None]]
    )
    cells = jnp.stack(
        [
            positions[0],
            positions[1],
            velocity[0],
            velocity[1],
            density,
            pressure_ratio(density),
            grad_coef * (particle_mass * live),
            live,
        ],
        axis=2,
    )
    cells = padded(cells, (("shore", 0), ("cross", 1)))
    counts = jnp.sum(cells[:, :, 7, :], axis=2).astype(jnp.int32)
    moved, peak = all_forces(counts, wind_table, cells, wind_seed, live, base)
    got, top = exchange(groups, migrant_count[0, 0], migrant_slot[0, 0], base, moved, peak)
    return advance(top, base, moved, got)


def solution(mesh):
    shores, crosses = mesh.shape["shore"], mesh.shape["cross"]
    groups = (8, shores // 8, 8, crosses // 8)
    lined = P("shore", "cross", None)
    return jax.shard_map(
        functools.partial(body, groups),
        mesh=mesh,
        in_specs=(
            P(None, "shore", "cross", None),
            P(None, "shore", "cross", None),
            lined,
            lined,
            P("shore", "cross"),
            lined,
            P(),
            P("shore", "cross", None, None),
            lined,
        ),
        out_specs=(P(None, "shore", "cross", None), P("shore", "cross", None, None, None)),
        check_vma=False,
    )
```

time: 341 us -> 176 us (0.52); the launches traced: 336 us -> 176 us
  Pallas kernels: 0 us -> 145 us
  other arithmetic: 131 us -> 2.61 us
  blocking collectives: 69.4 us -> 0 us
  local copies, waits for them, and re-layouts: 51.9 us -> 7.02 us
  loops' own time: 33.5 us -> 0 us
  starting transfers between devices: 36 us -> 16.3 us
  waiting for transfers between devices: 11.2 us -> 4.19 us
    pallas_call x0 -> x3, Pallas kernels: none -> 145 us  [the longest x1 92.8 us: all_forces(): pl.pallas_call(force_kernel, out_shape=(jax.ShapeDtypeStruct((3, rows, co...]
    reduce_sum x64 -> x1, other arithmetic: 123 us -> 0.11 us  [body(): counts = jnp.sum(cells[:, :, 7, :], axis=2).astype(jnp.int32)]
    pmax x5 -> x0, blocking collectives: 69.4 us -> none  [one_axis_at_a_time(): return functools.reduce(lax.pmax, axes, array)]
    another operation x1 -> x0, loops' own time: 33.5 us -> none  [half_forces(): lax.map(one_row, jnp.arange(row_count, dtype=jnp.int32))]
    gather x2 -> x0, local copies, waits for them, and re-layouts: 30.1 us -> none  [pick_migrants(): picked = jnp.take(flattened, slot_list.reshape(-1), axis=1)]
    ppermute x11 -> x4, starting transfers between devices: 36 us -> 16.3 us  [the longest x2 10.5 us: padded(): lax.ppermute(head, axis, [(i + 1, i) for i in range(ends)])]
    dynamic_slice x16 -> x0, local copies, waits for them, and re-layouts: 9.38 us -> none  [half_forces(): lax.map(one_row, jnp.arange(row_count, dtype=jnp.int32))]
    ppermute x11 -> x4, waiting for transfers between devices: 11.2 us -> 4.19 us  [the longest x2 4 us: padded(): lax.ppermute(head, axis, [(i + 1, i) for i in range(ends)])]
  transfers between devices with their start and end apart: 11 -> 4, of which waited for: 5 -> 3; matrix products, arithmetic and copies ran while one was open for 1% -> 0% of each run, Pallas kernels for 0% -> 0%
where the time goes in v1:
time: 176 us
  Pallas kernels  145 us (82%)
  starting transfers between devices  16.3 us (9%)
  local copies, waits for them, and re-layouts  7.02 us (4%)
  waiting for transfers between devices  4.19 us (2%)
  other arithmetic  2.61 us (1%)
    pallas_call x1, Pallas kernels, all_forces(): pl.pallas_call(force_kernel, out_shape=(jax.ShapeDtypeStruct((3, rows, co...  92.8 us
    pallas_call x1, Pallas kernels, exchange(): pl.pallas_call(functools.partial(exchange_kernel, groups), out_shape=(jax...  49.6 us
    ppermute x2, starting transfers between devices, padded(): lax.ppermute(head, axis, [(i + 1, i) for i in range(ends)])  10.5 us
    unnamed x24, local copies, waits for them, and re-layouts  6.59 us
    ppermute x2, starting transfers between devices, padded(): lax.ppermute(tail, axis, [(i, i + 1) for i in range(ends)])  5.79 us
    ppermute x2, waiting for transfers between devices, padded(): lax.ppermute(head, axis, [(i + 1, i) for i in range(ends)])  4 us
  transfers between devices with their start and end apart: 4, of which 3 were waited for; matrix products, arithmetic and copies ran while one was open for 0% of the time, Pallas kernels for 0%

profile of v1, /device:TPU:1, one launch (start us, length us, event | category | flops | bytes accessed | tf_op | source)
XLA Modules:
  0.0 175.6 jit_solution(8498796422823476510)
XLA Ops:
  0.6 0.0 copy-start.6
  0.6 0.0 copy-start.7
  0.7 0.0 copy-start.5
  0.7 0.0 copy-start.8
  0.7 0.8 copy.11
  1.5 0.8 bitcast_dynamic-update-slice_fusion.5
  2.3 0.8 bitcast_dynamic-update-slice_fusion.4
  3.2 0.8 bitcast_dynamic-update-slice_fusion.3
  4.0 0.8 bitcast_dynamic-update-slice_fusion.2
  4.9 0.8 bitcast_dynamic-update-slice_fusion.1
  5.7 0.9 fusion.6
  6.6 0.9 bitcast_dynamic-update-slice_fusion
  7.5 0.1 convert_dynamic-update-slice_fusion
  7.6 4.5 %collective-permute-start = (f32[1,8,8,128]{3,1,0,2:T(8,128)S(1)}, f32[1,8,8,128]{3,1,0,2:T(8,128)S(1)}, u32[]{:S(2)}, u32[]{:S(2)}) collective-permute-start(f32[1,8,8,128]{3,1,0,2:T(8,128)S(1)} %get-tuple-element.12), channel_id=1, source_target_pairs={{0,32},{32,64},{64,96},{96,128},{128,160},{160,192},{192,224},{224... | collective-permute-start | bytes 98312 | tf_op jit(solution)/shard_map/ppermute | solution.py:38
  12.1 9.2 %collective-permute-start.1 = (f32[1,8,8,128]{3,1,0,2:T(8,128)S(1)}, f32[1,8,8,128]{3,1,0,2:T(8,128)S(1)}, u32[]{:S(2)}, u32[]{:S(2)}) collective-permute-start(f32[1,8,8,128]{3,1,0,2:T(8,128)S(1)} %get-tuple-element.13), channel_id=1, source_target_pairs={{32,0},{64,32},{96,64},{128,96},{160,128},{192,160},{224,192},{256... | collective-permute-start | bytes 98312 | tf_op jit(solution)/shard_map/ppermute | solution.py:40
  21.3 0.1 fusion.8.live_ref
  21.4 0.0 copy-done.5
  21.4 0.0 copy-done.8
  21.4 0.1 select_bitcast_fusion
  21.6 0.0 copy-done.6
  21.6 0.0 copy-done.7
  21.6 0.1 fusion.pick_ref
  21.7 0.0 collective-permute-done
  21.7 0.4 collective-permute-done.1
  22.2 0.1 pad_maximum_fusion.4
  22.2 1.3 collective-permute-start.2
  23.5 1.3 collective-permute-start.3
  24.9 0.0 copy-start
  24.9 0.2 collective-permute-done.2
  25.1 3.6 %collective-permute-done.3 = f32[18,1,8,128]{3,1,0,2:T(1,128)S(1)} collective-permute-done((f32[18,1,8,128]{3,1,0,2:T(1,128)S(1)}, f32[18,1,8,128]{3,1,0,2:T(1,128)S(1)}, u32[]{:S(2)}, u32[]{:S(2)}) %collective-permute-start.3) | collective-permute-done | bytes 73760 | tf_op jit(solution)/shard_map/ppermute | solution.py:40
  28.6 0.2 pad_maximum_fusion
  28.9 0.0 copy-start.2
  28.9 0.0 copy-start.4
  28.9 0.4 copy.13.cells_ref
  29.3 0.1 slice_reduce_fusion
  29.5 0.0 copy-done
  29.5 0.2 copy-done.2
  29.7 0.0 copy-done.4
  29.7 92.8 %shard_map.104 = (f32[3,16,8,128]{3,2,1,0:T(8,128)S(1)}, f32[8,128]{1,0:T(8,128)S(1)}) custom-call(s32[18,10]{1,0:T(8,128)S(1)} %convert_element_type.13.counts_ref, f32[2,16]{1,0:T(2,128)S(1)} %copy-done.4, f32[18,10,8,128]{3,2,1,0:T(8,128)S(1)} %copy.13.cells_ref, bf16[24,896]{1,0:T(8,128)(2,1)S(1)} %fusion.pick_ref, s32[16,8,128]{2,1,0:T(8,128)S(1)} %copy-done.2, ...), custom_call_target="tpu_custom_call" | custom-call | tf_op jit(solution)/shard_map/pallas_call | solution.py:174
  122.5 0.0 copy-start.1
  122.6 0.7 copy-done.1
  123.2 0.0 copy-start.3
  123.2 0.6 copy-done.3
  123.8 49.6 %shard_map.105 = (f32[4,9,1792]{2,1,0:T(8,128)}, f32[8,128]{1,0:T(8,128)}) custom-call(s32[4]{0:T(128)} %bitcast.23, s32[4,1792]{1,0:T(4,128)} %bitcast.22, f32[6,16,8,128]{3,2,1,0:T(8,128)} %copy-done, f32[3,16,8,128]{3,2,1,0:T(8,128)} %copy-done.1, f32[8,128]{1,0:T(8,128)} %copy-done.3), custom_call_target="tpu_custom_call" | custom-call | tf_op jit(solution)/shard_map/pallas_call | solution.py:320
  173.4 2.3 %shard_map.106 = (f32[7,16,8,128]{3,2,1,0:T(8,128)}, f32[1,1,4,8,1792]{4,3,2,1,0:T(8,128)}) custom-call(f32[8,128]{1,0:T(8,128)} %get-tuple-element.8.top_ref, f32[6,16,8,128]{3,2,1,0:T(8,128)} %copy-done, f32[3,16,8,128]{3,2,1,0:T(8,128)} %copy-done.1, f32[4,9,1792]{2,1,0:T(8,128)} %get-tuple-element.9.got_ref), custom_call_target="tpu_custom_call" | custom-call | tf_op jit(solution)/shard_map/pallas_call | solution.py:363
  (8 shorter events, 0.1 us)
Async XLA Ops:
  0.6 20.9 %copy-start.6 = (f32[2,16,8,128]{3,2,1,0:T(8,128)S(1)}, f32[2,16,8,128]{3,2,1,0:T(8,128)}, u32[]{:S(2)}) copy-start(f32[2,16,8,128]{3,2,1,0:T(8,128)} %param.9) | copy-start | bytes 393220
  0.6 20.9 %copy-start.7 = (f32[2,16,8,128]{3,2,1,0:T(8,128)S(1)}, f32[2,16,8,128]{3,2,1,0:T(8,128)}, u32[]{:S(2)}) copy-start(f32[2,16,8,128]{3,2,1,0:T(8,128)} %param.10) | copy-start | bytes 393220
  0.7 20.8 %copy-start.5 = (f32[16,8,128]{2,1,0:T(8,128)S(1)}, f32[16,8,128]{2,1,0:T(8,128)}, u32[]{:S(2)}) copy-start(f32[16,8,128]{2,1,0:T(8,128)} %param.11) | copy-start | bytes 196612
  0.7 20.8 %copy-start.8 = (f32[16,8,128]{2,1,0:T(8,128)S(1)}, f32[16,8,128]{2,1,0:T(8,128)}, u32[]{:S(2)}) copy-start(f32[16,8,128]{2,1,0:T(8,128)} %param.12) | copy-start | bytes 196612
  7.6 14.1 %collective-permute-start = (f32[1,8,8,128]{3,1,0,2:T(8,128)S(1)}, f32[1,8,8,128]{3,1,0,2:T(8,128)S(1)}, u32[]{:S(2)}, u32[]{:S(2)}) collective-permute-start(f32[1,8,8,128]{3,1,0,2:T(8,128)S(1)} %get-tuple-element.12), channel_id=1, source_target_pairs={{0,32},{32,64},{64,96},{96,128},{128,160},{160,192},{192,224},{224... | collective-permute-start | bytes 98312 | tf_op jit(solution)/shard_map/ppermute | solution.py:38
  12.1 10.0 %collective-permute-start.1 = (f32[1,8,8,128]{3,1,0,2:T(8,128)S(1)}, f32[1,8,8,128]{3,1,0,2:T(8,128)S(1)}, u32[]{:S(2)}, u32[]{:S(2)}) collective-permute-start(f32[1,8,8,128]{3,1,0,2:T(8,128)S(1)} %get-tuple-element.13), channel_id=1, source_target_pairs={{32,0},{64,32},{96,64},{128,96},{160,128},{192,160},{224,192},{256... | collective-permute-start | bytes 98312 | tf_op jit(solution)/shard_map/ppermute | solution.py:40
  22.2 2.8 %collective-permute-start.2 = (f32[18,1,8,128]{3,1,0,2:T(1,128)S(1)}, f32[18,1,8,128]{3,1,0,2:T(1,128)S(1)}, u32[]{:S(2)}, u32[]{:S(2)}) collective-permute-start(f32[18,1,8,128]{3,1,0,2:T(1,128)S(1)} %get-tuple-element.10), channel_id=1, source_target_pairs={{0,1},{1,2},{2,3},{3,4},{4,5},{5,6},{6,7},{7,8},{8,9},{9,10},{10,1... | collective-permute-start | bytes 221192 | tf_op jit(solution)/shard_map/ppermute | solution.py:38
  23.5 5.1 %collective-permute-start.3 = (f32[18,1,8,128]{3,1,0,2:T(1,128)S(1)}, f32[18,1,8,128]{3,1,0,2:T(1,128)S(1)}, u32[]{:S(2)}, u32[]{:S(2)}) collective-permute-start(f32[18,1,8,128]{3,1,0,2:T(1,128)S(1)} %get-tuple-element.11), channel_id=1, source_target_pairs={{1,0},{2,1},{3,2},{4,3},{5,4},{6,5},{7,6},{8,7},{9,8},{10,9},{11,1... | collective-permute-start | bytes 221192 | tf_op jit(solution)/shard_map/ppermute | solution.py:40
  24.9 4.6 %copy-start = (f32[6,16,8,128]{3,2,1,0:T(8,128)}, f32[6,16,8,128]{3,2,1,0:T(8,128)S(1)}, u32[]{:S(2)}) copy-start(f32[6,16,8,128]{3,2,1,0:T(8,128)S(1)} %pad_maximum_fusion.1.base_ref) | copy-start | bytes 1179652
  28.9 0.8 copy-start.2
  28.9 0.8 copy-start.4
  122.5 0.7 copy-start.1
  123.2 0.6 copy-start.3

commit v2 on v1

--- a/solution.py
+++ b/solution.py
@@ -28,20 +28,101 @@
     return pressure / (density * density)
 
 
-def padded(cells, sides):
-    for axis, dim in sides:
-        ends = lax.axis_size(axis) - 1
-        head = lax.slice_in_dim(cells, 0, 1, axis=dim)
-        tail = lax.slice_in_dim(cells, cells.shape[dim] - 1, cells.shape[dim], axis=dim)
-        cells = jnp.concatenate(
-            [
-                lax.ppermute(tail, axis, [(i, i + 1) for i in range(ends)]),
-                cells,
-                lax.ppermute(head, axis, [(i + 1, i) for i in range(ends)]),
-            ],
-            axis=dim,
+def halo_kernel(
+    shores, crosses, count_ref, positions_ref, velocity_ref, density_ref, mass_ref, cells_ref, base_ref, live_ref, send, recv
+):
+    shore, cross = lax.axis_index("shore"), lax.axis_index("cross")
+    rows, cols = live_ref.shape[:2]
+    steps = [(dx, dy) for dx in (-1, 0, 1) for dy in (-1, 0, 1) if dx or dy]
+    barrier = pltpu.get_barrier_semaphore()
+    for dx, dy in steps:
+        peer = (lax.rem(shore + dx + shores, shores), lax.rem(cross + dy + crosses, crosses))
+        pl.semaphore_signal(barrier, inc=1, device_id=peer, device_id_type=MESH)
+
+    which = lax.broadcasted_iota(jnp.int32, (cols, LANES), 0)
+    slot = lax.broadcasted_iota(jnp.int32, (cols, LANES), 1)
+
+    @pl.loop(0, rows)
+    def _(row):
+        filled = jnp.full((cols, LANES), count_ref[row, 0], jnp.int32)
+        for col in range(1, cols):
+            filled = jnp.where(which == col, count_ref[row, col], filled)
+        live = jnp.where(slot < filled, 1.0, 0.0)
+        x, y, u, v = positions_ref[0, row], positions_ref[1, row], velocity_ref[0, row], velocity_ref[1, row]
+        dense = density_ref[row]
+        mass = mass_ref[row] * live
+        fields = (x, y, u, v, dense, pressure_ratio(dense), grad_coef * mass, live)
+        for f, value in enumerate(fields):
+            cells_ref[row + 1, 1 : cols + 1, f, :] = value
+        for f, value in enumerate((x * live, y * live, u * live, v * live, dense * live, mass)):
+            base_ref[f, row] = value
+        live_ref[row] = live
+
+    pl.semaphore_wait(barrier, len(steps))
+
+    def edge(step, count):
+        return pl.ds(1, count) if step == 0 else pl.ds(1 if step < 0 else count, 1)
+
+    def rim(step, count):
+        return pl.ds(1, count) if step == 0 else pl.ds(count + 1 if step < 0 else 0, 1)
+
+    def inside(dx, dy):
+        found = True
+        for at, step, ends in ((shore, dx, shores), (cross, dy, crosses)):
+            if step:
+                found = jnp.logical_and(found, at < ends - 1 if step > 0 else at > 0)
+        return found
+
+    def copy(k):
+        dx, dy = steps[k]
+        return pltpu.make_async_remote_copy(
+            src_ref=cells_ref.at[edge(dx, rows), edge(dy, cols)],
+            dst_ref=cells_ref.at[rim(dx, rows), rim(dy, cols)],
+            send_sem=send.at[k],
+            recv_sem=recv.at[k],
+            device_id=(shore + dx, cross + dy),
+            device_id_type=MESH,
         )
-    return cells
+
+    for k, (dx, dy) in enumerate(steps):
+
+        @pl.when(inside(dx, dy))
+        def _():
+            copy(k).start()
+
+    for k, (dx, dy) in enumerate(steps):
+
+        @pl.when(jnp.logical_not(inside(-dx, -dy)))
+        def _():
+            at = (rim(dx, rows), rim(dy, cols))
+            cells_ref[at] = jnp.zeros((at[0].size, at[1].size, SUB, LANES), jnp.float32)
+
+    for k, (dx, dy) in enumerate(steps):
+
+        @pl.when(inside(dx, dy))
+        def _():
+            copy(k).wait_send()
+
+        @pl.when(inside(-dx, -dy))
+        def _():
+            copy(k).wait_recv()
+
+
+def halo(shores, crosses, cell_count, positions, velocity, density, particle_mass):
+    rows, cols = density.shape[:2]
+    vmem = pl.BlockSpec(memory_space=pltpu.VMEM)
+    return pl.pallas_call(
+        functools.partial(halo_kernel, shores, crosses),
+        out_shape=(
+            jax.ShapeDtypeStruct((rows + 2, cols + 2, SUB, LANES), jnp.float32),
+            jax.ShapeDtypeStruct((6, rows, cols, LANES), jnp.float32),
+            jax.ShapeDtypeStruct((rows, cols, LANES), jnp.float32),
+        ),
+        in_specs=[pl.BlockSpec(memory_space=pltpu.SMEM)] + [vmem] * 4,
+        out_specs=(vmem,) * 3,
+        scratch_shapes=[pltpu.SemaphoreType.DMA((8,)), pltpu.SemaphoreType.DMA((8,))],
+        compiler_params=pltpu.CompilerParams(collective_id=1, has_side_effects=True),
+    )(cell_count, positions, velocity, density, particle_mass)
 
 
 def halves(exact, parts):
@@ -53,7 +134,7 @@
 
 
 def force_kernel(
-    counts_ref, table_ref, cells_ref, pick_ref, seed_ref, live_ref, base_ref, out_ref, peak_ref, placed, wide, sums
+    counts_ref, table_ref, cells_ref, pick_ref, seed_ref, live_ref, base_ref, out_ref, peak_ref, placed, wide, sums, returned
 ):
     height, width = cells_ref.shape[:2]
     rows, cols = height - 2, width - 2
@@ -81,61 +162,134 @@
                 preferred_element_type=jnp.float32,
             )
 
-    def one_cell(row, col, row_steps, col_steps):
+    def loop_over(row, col):
         count = lax.div(counts_ref[row, col] + (SUB * GROUP - 1), SUB * GROUP)
 
-        @pl.loop(0, count)
-        def _(part):
+        def loaded(part):
             near = []
             for g in range(GROUP):
                 at = pl.ds(pl.multiple_of((part * GROUP + g) * SUB, SUB), SUB)
                 near.append(tuple(wide[col, at, f * LANES : (f + 1) * LANES] for f in range(FIELDS)))
-            for dr in row_steps:
-                for dc in col_steps:
-                    xi, yi, ui, vi, di, pi = (
-                        jnp.broadcast_to(placed[row + dr, col + dc, f : f + 1, :], (SUB, LANES)) for f in range(6)
-                    )
-                    fx = fy = rate = None
-                    for g in range(GROUP):
-                        xj, yj, uj, vj, dj, pj, mj = near[g]
-                        ox = xi - xj
-                        oy = yi - yj
-                        d2 = ox * ox + oy * oy
-                        r = d2 * lax.rsqrt(jnp.maximum(d2, TINY))
-                        f = jnp.maximum(1.0 - r, 0.0)
-                        w = mj * (f * f * f)
-                        a = (ui - uj) * ox + (vi - vj) * oy
-                        q = (d2 + 0.01 * smooth * smooth) * (di + dj)
-                        c = w * ((pi + pj) - jnp.minimum(a, 0.0) * pl.reciprocal(q))
-                        fx = c * ox if g == 0 else fx + c * ox
-                        fy = c * oy if g == 0 else fy + c * oy
-                        rate = w * a if g == 0 else rate + w * a
-                    own = (row + dr - 1, col + dc - 1)
-                    sums[own[0], own[1], 0] += fx
-                    sums[own[0], own[1], 1] += fy
-                    sums[own[0], own[1], 2] += rate
-
-    def one_row(row, row_steps):
+            return near
+
+        return count, loaded
+
+    def shared(own, near):
+        xi, yi, ui, vi, di, pi = own
+        xj, yj, uj, vj, dj, pj = near
+        ox = xi - xj
+        oy = yi - yj
+        d2 = ox * ox + oy * oy
+        near_d2 = jnp.clip(d2, TINY, 1.0)
+        f = 1.0 - near_d2 * lax.rsqrt(near_d2)
+        f3 = f * f * f
+        a = (ui - uj) * ox + (vi - vj) * oy
+        q = (d2 + 0.01 * smooth * smooth) * (di + dj)
+        return ox, oy, f3, a, (pi + pj) - jnp.minimum(a, 0.0) * pl.reciprocal(q)
+
+    def row_of(row, col, f):
+        return jnp.broadcast_to(placed[row, col, f : f + 1, :], (SUB, LANES))
+
+    def plus(total, terms):
+        return terms if total is None else tuple(t + x for t, x in zip(total, terms))
+
+    def one_way(row, col, step, near):
+        own = (row + step[0], col + step[1])
+        fields = [row_of(own[0], own[1], f) for f in range(6)]
+        total = None
+        for there in near:
+            ox, oy, f3, a, c = shared(fields, there[:6])
+            w = there[6] * f3
+            c = w * c
+            total = plus(total, (c * ox, c * oy, w * a))
+        for k in range(3):
+            sums[own[0] - 1, own[1] - 1, k] += total[k]
+
+    def both_ways(row, col, step, near, back):
+        own = (row + step[0], col + step[1])
+        fields = [row_of(own[0], own[1], f) for f in range(6)]
+        mass = row_of(own[0], own[1], 6)
+        total = None
+        for g, there in enumerate(near):
+            ox, oy, f3, a, c = shared(fields, there[:6])
+            c = f3 * c
+            terms = (c * ox, c * oy, f3 * a)
+            total = plus(total, tuple(there[6] * t for t in terms))
+            back[g] = plus(back[g], tuple(mass * t for t in terms))
+        for k in range(3):
+            sums[own[0] - 1, own[1] - 1, k] += total[k]
+
+    def outer_cell(row, col, steps):
+        count, loaded = loop_over(row, col)
+
+        @pl.loop(0, count)
+        def _(part):
+            near = loaded(part)
+            for step in steps:
+                one_way(row, col, step, near)
+
+    def inner_cell(row, col, steps):
+        count, loaded = loop_over(row, col)
+
+        @pl.loop(0, count)
+        def _(part):
+            near = loaded(part)
+            back = [None] * GROUP
+            one_way(row, col, (0, 0), near)
+            for step in steps:
+                both_ways(row, col, step, near, back)
+            for g in range(GROUP):
+                if back[g] is not None:
+                    at = pl.ds(pl.multiple_of((part * GROUP + g) * SUB, SUB), SUB)
+                    for k in range(3):
+                        returned[col - 1, k, at, :] = back[g][k]
+
+    def outer_row(row, step):
         widen(row)
-        one_cell(row, 0, row_steps, (1,))
-        one_cell(row, 1, row_steps, (0, 1))
+        outer_cell(row, 0, ((step, 1),))
+        outer_cell(row, 1, ((step, 0), (step, 1)))
 
         @pl.loop(2, width - 2)
         def _(col):
-            one_cell(row, col, row_steps, (-1, 0, 1))
-
-        one_cell(row, width - 2, row_steps, (-1, 0))
-        one_cell(row, width - 1, row_steps, (-1,))
-
-    one_row(0, (1,))
-    one_row(1, (0, 1))
+            outer_cell(row, col, ((step, -1), (step, 0), (step, 1)))
+
+        outer_cell(row, width - 2, ((step, -1), (step, 0)))
+        outer_cell(row, width - 1, ((step, -1),))
+
+    def inner_row(row, drs, last):
+        widen(row)
+        outer_cell(row, 0, tuple((dr, 1) for dr in drs))
+        outer_cell(row, width - 1, tuple((dr, -1) for dr in drs))
+        down = () if last else ((1, -1), (1, 0), (1, 1))
+        inner_cell(row, 1, ((0, 1),) + down[1:])
+
+        @pl.loop(2, width - 2)
+        def _(col):
+            inner_cell(row, col, ((0, 1),) + down)
+
+        inner_cell(row, width - 2, down[:2])
+        for col in range(cols - 1 if last else cols):
+            for k in range(3):
+                turned = jnp.transpose(returned[col, k])
+                total = turned[0:SUB]
+                for v in range(1, LANES // SUB):
+                    total = total + turned[v * SUB : (v + 1) * SUB]
+                sums[row - 1, col, k] += total if k == 2 else -total
+
+    @pl.loop(0, cols)
+    def _(col):
+        for k in range(3):
+            returned[col, k] = jnp.zeros((LANES, LANES), jnp.float32)
+
+    outer_row(0, 1)
+    inner_row(1, (0, 1), False)
 
     @pl.loop(2, height - 2)
     def _(row):
-        one_row(row, (-1, 0, 1))
-
-    one_row(height - 2, (-1, 0))
-    one_row(height - 1, (-1,))
+        inner_row(row, (-1, 0, 1), False)
+
+    inner_row(height - 2, (-1, 0), True)
+    outer_row(height - 1, -1)
 
     def finish(row, peaks):
         live = live_ref[row]
@@ -183,6 +337,7 @@
             pltpu.VMEM((height, width, SUB, LANES), jnp.float32),
             pltpu.VMEM((width, LANES, FIELDS * LANES), jnp.float32),
             pltpu.VMEM((rows, cols, 3, SUB, LANES), jnp.float32),
+            pltpu.VMEM((cols, 3, LANES, LANES), jnp.float32),
         ],
         compiler_params=pltpu.CompilerParams(vmem_limit_bytes=32 << 20),
     )(counts, table, cells, pick, seed, live, base)
@@ -190,7 +345,7 @@
 
 def exchange_kernel(
     groups, counts_ref, slots_ref, base_ref, moved_ref, peak_ref, got_ref, top_ref,
-    split, leaving, held, heap_a, heap_b, heap_c, send_a, recv_a, send_b, recv_b, send_c, recv_c, send_m, recv_m,
+    split, found, leaving, held, heap_a, heap_b, heap_c, send_a, recv_a, send_b, recv_b, send_c, recv_c, send_m, recv_m,
 ):
     inner, outer, near, far = groups
     shore, cross = lax.axis_index("shore"), lax.axis_index("cross")
@@ -234,23 +389,24 @@
 
     width = slots_ref.shape[1]
     rank = lax.broadcasted_iota(jnp.int32, (LANES, TILE), 0)
-    for d in range(4):
-
+
+    def gather(d):
         @pl.loop(0, width // TILE)
         def _(t):
             at = pl.ds(pl.multiple_of(t * TILE, TILE), TILE)
             slot = slots_ref[d : d + 1, at]
             lane = jnp.where(rank == (slot & (LANES - 1)), 1.0, 0.0)
             lanes = jnp.concatenate([lane, lane], axis=0).astype(jnp.bfloat16)
+            found[...] = jnp.dot(split[...], lanes, preferred_element_type=jnp.float32)
             order = lax.broadcasted_iota(jnp.int32, (1, TILE), 1) + t * TILE
             cell = jnp.where(order < counts_ref[d], lax.shift_right_logical(slot, 7), -1)
             keep = rank == cell
             for f in range(kinds):
-                found = jnp.dot(
-                    split[f * cells : (f + 1) * cells, :], lanes, preferred_element_type=jnp.float32
-                )
-                leaving[d, f : f + 1, at] = jnp.sum(jnp.where(keep, found, 0.0), axis=0, keepdims=True)
-
+                mine = found[f * cells : (f + 1) * cells, :]
+                leaving[d, f : f + 1, at] = jnp.sum(jnp.where(keep, mine, 0.0), axis=0, keepdims=True)
+
+    gather(0)
+    gather(1)
     pl.semaphore_wait(barrier, len(greeted))
 
     def migrants(d):
@@ -265,6 +421,7 @@
 
     held[0] = peak_ref[...]
     stages = ((along, heap_a, send_a, recv_a), (across, heap_b, send_b, recv_b), (depth, heap_c, send_c, recv_c))
+    ready = ((0, 1, 2), (3,), ())
     for step, (peers, heap, send, recv) in enumerate(stages):
         copies = [
             pltpu.make_async_remote_copy(
@@ -279,12 +436,13 @@
         ]
         for copy in copies:
             copy.start()
-        if step == 0:
-            for d in range(4):
-
-                @pl.when(ends[d][0])
-                def _():
-                    migrants(d).start()
+        for d in ready[step]:
+            if d > 1:
+                gather(d)
+
+            @pl.when(ends[d][0])
+            def _():
+                migrants(d).start()
 
         top = held[step]
         for o, copy in enumerate(copies):
@@ -327,6 +485,7 @@
         out_specs=(pl.BlockSpec(memory_space=pltpu.VMEM),) * 2,
         scratch_shapes=[
             pltpu.VMEM((kinds * cells, 2 * LANES), jnp.bfloat16),
+            pltpu.VMEM((kinds * cells, TILE), jnp.float32),
             pltpu.VMEM((4, kinds, width), jnp.float32),
             pltpu.VMEM((4, SUB, LANES), jnp.float32),
             pltpu.VMEM((inner - 1, SUB, LANES), jnp.float32),
@@ -374,25 +533,10 @@
 def body(
     groups, positions, velocity, density, particle_mass, cell_count, wind_seed, wind_table, migrant_slot, migrant_count
 ):
-    slot_ids = jnp.arange(positions.shape[3], dtype=jnp.int32)
-    live = (slot_ids[None, None, :] < cell_count[:, :, None]).astype(jnp.float32)
-    base = jnp.concatenate(
-        [positions * live, velocity * live, (density * live)[None], (particle_mass * live)[None]]
+    inner, outer, near, far = groups
+    cells, base, live = halo(
+        inner * outer, near * far, cell_count, positions, velocity, density, particle_mass
     )
-    cells = jnp.stack(
-        [
-            positions[0],
-            positions[1],
-            velocity[0],
-            velocity[1],
-            density,
-            pressure_ratio(density),
-            grad_coef * (particle_mass * live),
-            live,
-        ],
-        axis=2,
-    )
-    cells = padded(cells, (("shore", 0), ("cross", 1)))
     counts = jnp.sum(cells[:, :, 7, :], axis=2).astype(jnp.int32)
     moved, peak = all_forces(counts, wind_table, cells, wind_seed, live, base)
     got, top = exchange(groups, migrant_count[0, 0], migrant_slot[0, 0], base, moved, peak)

time: 176 us -> 141 us (0.80)
  starting transfers between devices: 16.3 us -> 0 us
  Pallas kernels: 145 us -> 132 us
  waiting for transfers between devices: 4.19 us -> 0 us
    pallas_call x0 -> x1, Pallas kernels: none -> 23.2 us  [halo(): pl.pallas_call(functools.partial(halo_kernel, shores, crosses), out_shape...]
    pallas_call x1, Pallas kernels: 49.6 us -> 27.6 us  [exchange(): pl.pallas_call(functools.partial(exchange_kernel, groups), out_shape=(jax...]
    ppermute x4 -> x0, starting transfers between devices: 16.3 us -> none  [the longest x2 10.5 us: padded(): lax.ppermute(head, axis, [(i + 1, i) for i in range(ends)])]
    pallas_call x1, Pallas kernels: 92.8 us -> 79 us  [all_forces(): pl.pallas_call(force_kernel, out_shape=(jax.ShapeDtypeStruct((3, rows, co...]
    ppermute x4 -> x0, waiting for transfers between devices: 4.19 us -> none  [the longest x2 4 us: padded(): lax.ppermute(head, axis, [(i + 1, i) for i in range(ends)])]
    unnamed x2 -> x0, other arithmetic: 1.79 us -> none
    unnamed x24 -> x17, local copies, waits for them, and re-layouts: 6.59 us -> 5.34 us
  transfers between devices with their start and end apart: 4 -> 0, of which waited for: 3 -> 0; matrix products, arithmetic and copies ran while one was open for 0% -> 0% of each run, Pallas kernels for 0% -> 0%
where the time goes in v2:
time: 141 us; the launch traced here: 140 us
  Pallas kernels  132 us (94%)
  local copies, waits for them, and re-layouts  5.34 us (4%)
  other arithmetic  1.66 us (1%)
    pallas_call x1, Pallas kernels, all_forces(): pl.pallas_call(force_kernel, out_shape=(jax.ShapeDtypeStruct((3, rows, co...  79 us
    pallas_call x1, Pallas kernels, exchange(): pl.pallas_call(functools.partial(exchange_kernel, groups), out_shape=(jax...  27.6 us
    pallas_call x1, Pallas kernels, halo(): pl.pallas_call(functools.partial(halo_kernel, shores, crosses), out_shape...  23.2 us
    unnamed x17, local copies, waits for them, and re-layouts  5.34 us

profile of v2, /device:TPU:1, one launch (start us, length us, event | category | flops | bytes accessed | tf_op | source)
XLA Modules:
  0.0 139.9 jit_solution(7679976806144112149)
XLA Ops:
  0.6 0.0 copy-start.7
  0.7 0.7 copy-done.7
  1.3 0.7 copy.11.count_ref
  2.0 0.1 fusion.pick_ref
  2.1 23.2 %shard_map.104 = (f32[18,10,8,128]{3,2,1,0:T(8,128)}, f32[6,16,8,128]{3,2,1,0:T(8,128)}, f32[16,8,128]{2,1,0:T(8,128)}) custom-call(s32[16,8]{1,0:T(8,128)} %copy.11.count_ref, f32[2,16,8,128]{3,2,1,0:T(8,128)} %positions_ref.1, f32[2,16,8,128]{3,2,1,0:T(8,128)} %velocity_ref.1, f32[16,8,128]{2,1,0:T(8,128)} %density_ref.1, f32[16,8,128]{2,1,0:T(8,128)} %mass_ref.1), custom_call_target="tpu_custom_call" | custom-call | tf_op jit(solution)/shard_map/pallas_call | solution.py:114
  25.3 0.0 copy-start.4
  25.3 0.0 copy-start.3
  25.3 1.6 %slice_reduce_fusion = f32[18,10]{1,0:T(8,128)S(1)} fusion(f32[18,10,8,128]{3,2,1,0:T(8,128)} %get-tuple-element.10.cells_ref), kind=kLoop, calls=%fused_computation | loop fusion | flops 22860 | bytes 92880 | tf_op jit(solution)/shard_map/reduce_sum | solution.py:540
  26.9 0.0 copy-start.6
  26.9 0.0 copy-done.4
  26.9 0.0 copy-done.3
  26.9 0.6 copy-done.6
  27.6 0.0 copy-start
  27.6 1.0 copy-done
  28.6 0.0 copy-start.1
  28.6 1.1 copy-done.1
  29.7 79.0 %shard_map.105 = (f32[3,16,8,128]{3,2,1,0:T(8,128)S(1)}, f32[8,128]{1,0:T(8,128)S(1)}) custom-call(s32[18,10]{1,0:T(8,128)S(1)} %convert_element_type.6.counts_ref, f32[2,16]{1,0:T(2,128)S(1)} %copy-done.6, f32[18,10,8,128]{3,2,1,0:T(8,128)S(1)} %copy-done.1, bf16[24,896]{1,0:T(8,128)(2,1)S(1)} %fusion.pick_ref, s32[16,8,128]{2,1,0:T(8,128)S(1)} %copy-done.3, ...), custom_call_target="tpu_custom_call" | custom-call | tf_op jit(solution)/shard_map/pallas_call | solution.py:328
  108.7 0.0 copy-start.2
  108.7 0.7 copy-done.2
  109.3 0.0 copy-start.5
  109.4 0.6 copy-done.5
  109.9 27.6 %shard_map.106 = (f32[4,9,1792]{2,1,0:T(8,128)}, f32[8,128]{1,0:T(8,128)}) custom-call(s32[4]{0:T(128)} %bitcast.3, s32[4,1792]{1,0:T(4,128)} %bitcast.2, f32[6,16,8,128]{3,2,1,0:T(8,128)} %get-tuple-element.9.base_ref, f32[3,16,8,128]{3,2,1,0:T(8,128)} %copy-done.2, f32[8,128]{1,0:T(8,128)} %copy-done.5), custom_call_target="tpu_custom_call" | custom-call | tf_op jit(solution)/shard_map/pallas_call | solution.py:478
  137.6 2.3 %shard_map.107 = (f32[7,16,8,128]{3,2,1,0:T(8,128)}, f32[1,1,4,8,1792]{4,3,2,1,0:T(8,128)}) custom-call(f32[8,128]{1,0:T(8,128)} %get-tuple-element.14.top_ref, f32[6,16,8,128]{3,2,1,0:T(8,128)} %get-tuple-element.9.base_ref, f32[3,16,8,128]{3,2,1,0:T(8,128)} %copy-done.2, f32[4,9,1792]{2,1,0:T(8,128)} %get-tuple-element.15.got_ref), custom_call_target="tpu_custom_call" | custom-call | tf_op jit(solution)/shard_map/pallas_call | solution.py:522
  (5 shorter events, 0.0 us)
Async XLA Ops:
  0.6 0.7 copy-start.7
  25.3 1.6 %copy-start.4 = (f32[16,8,128]{2,1,0:T(8,128)S(1)}, f32[16,8,128]{2,1,0:T(8,128)}, u32[]{:S(2)}) copy-start(f32[16,8,128]{2,1,0:T(8,128)} %get-tuple-element.11.live_ref) | copy-start | bytes 196612
  25.3 1.6 %copy-start.3 = (s32[16,8,128]{2,1,0:T(8,128)S(1)}, s32[16,8,128]{2,1,0:T(8,128)}, u32[]{:S(2)}) copy-start(s32[16,8,128]{2,1,0:T(8,128)} %seed_ref.1) | copy-start | bytes 196612
  26.9 0.7 copy-start.6
  27.6 1.0 copy-start
  28.6 1.1 copy-start.1
  108.7 0.7 copy-start.2
  109.3 0.6 copy-start.5

commit v3 on v2

--- a/solution.py
+++ b/solution.py
@@ -29,10 +29,10 @@
 
 
 def halo_kernel(
-    shores, crosses, count_ref, positions_ref, velocity_ref, density_ref, mass_ref, cells_ref, base_ref, live_ref, send, recv
+    shores, crosses, count_ref, positions_ref, velocity_ref, density_ref, mass_ref, cells_ref, base_ref, speed_ref, send, recv
 ):
     shore, cross = lax.axis_index("shore"), lax.axis_index("cross")
-    rows, cols = live_ref.shape[:2]
+    rows, cols = density_ref.shape[:2]
     steps = [(dx, dy) for dx in (-1, 0, 1) for dy in (-1, 0, 1) if dx or dy]
     barrier = pltpu.get_barrier_semaphore()
     for dx, dy in steps:
@@ -42,8 +42,7 @@
     which = lax.broadcasted_iota(jnp.int32, (cols, LANES), 0)
     slot = lax.broadcasted_iota(jnp.int32, (cols, LANES), 1)
 
-    @pl.loop(0, rows)
-    def _(row):
+    def pack(row, fastest):
         filled = jnp.full((cols, LANES), count_ref[row, 0], jnp.int32)
         for col in range(1, cols):
             filled = jnp.where(which == col, count_ref[row, col], filled)
@@ -56,7 +55,10 @@
             cells_ref[row + 1, 1 : cols + 1, f, :] = value
         for f, value in enumerate((x * live, y * live, u * live, v * live, dense * live, mass)):
             base_ref[f, row] = value
-        live_ref[row] = live
+        return jnp.maximum(fastest, (u * u + v * v) * live)
+
+    fastest = lax.fori_loop(0, rows, pack, jnp.zeros((cols, LANES), jnp.float32))
+    speed_ref[...] = jnp.full((SUB, LANES), jnp.max(fastest), jnp.float32)
 
     pl.semaphore_wait(barrier, len(steps))
 
@@ -116,7 +118,7 @@
         out_shape=(
             jax.ShapeDtypeStruct((rows + 2, cols + 2, SUB, LANES), jnp.float32),
             jax.ShapeDtypeStruct((6, rows, cols, LANES), jnp.float32),
-            jax.ShapeDtypeStruct((rows, cols, LANES), jnp.float32),
+            jax.ShapeDtypeStruct((SUB, LANES), jnp.float32),
         ),
         in_specs=[pl.BlockSpec(memory_space=pltpu.SMEM)] + [vmem] * 4,
         out_specs=(vmem,) * 3,
@@ -134,7 +136,7 @@
 
 
 def force_kernel(
-    counts_ref, table_ref, cells_ref, pick_ref, seed_ref, live_ref, base_ref, out_ref, peak_ref, placed, wide, sums, returned
+    table_ref, cells_ref, pick_ref, seed_ref, out_ref, peak_ref, placed, wide, sums, returned, counts
 ):
     height, width = cells_ref.shape[:2]
     rows, cols = height - 2, width - 2
@@ -152,18 +154,32 @@
             for c in range(3):
                 sums[row, col, c] = jnp.zeros((SUB, LANES), jnp.float32)
 
-    def widen(row):
+    def widen(row, col):
+        counts[row, col] = jnp.sum(cells_ref[row, col, 7:8, :]).astype(jnp.int32)
+        split = jnp.concatenate([x.astype(jnp.float32) for x in halves(placed[row, col], 3)], axis=0)
+        wide[col] = lax.dot_general(
+            jnp.transpose(split).astype(jnp.bfloat16),
+            pick_ref[...],
+            (((1,), (0,)), ((), ())),
+            preferred_element_type=jnp.float32,
+        )
+
+    def gather_back(row, col):
+        for k in range(3):
+            turned = jnp.transpose(returned[col, k])
+            total = turned[0:SUB]
+            for v in range(1, LANES // SUB):
+                total = total + turned[v * SUB : (v + 1) * SUB]
+            sums[row - 1, col, k] += total if k == 2 else -total
+
+    def turn(row, gathered):
         for col in range(width):
-            split = jnp.concatenate([x.astype(jnp.float32) for x in halves(placed[row, col], 3)], axis=0)
-            wide[col] = lax.dot_general(
-                jnp.transpose(split).astype(jnp.bfloat16),
-                pick_ref[...],
-                (((1,), (0,)), ((), ())),
-                preferred_element_type=jnp.float32,
-            )
+            widen(row + 1, col)
+            if col < gathered:
+                gather_back(row, col)
 
     def loop_over(row, col):
-        count = lax.div(counts_ref[row, col] + (SUB * GROUP - 1), SUB * GROUP)
+        count = lax.div(counts[row, col] + (SUB * GROUP - 1), SUB * GROUP)
 
         def loaded(part):
             near = []
@@ -196,10 +212,11 @@
     def one_way(row, col, step, near):
         own = (row + step[0], col + step[1])
         fields = [row_of(own[0], own[1], f) for f in range(6)]
+        mass = row_of(own[0], own[1], 6)
         total = None
         for there in near:
             ox, oy, f3, a, c = shared(fields, there[:6])
-            w = there[6] * f3
+            w = mass * there[6] * f3
             c = w * c
             total = plus(total, (c * ox, c * oy, w * a))
         for k in range(3):
@@ -212,10 +229,11 @@
         total = None
         for g, there in enumerate(near):
             ox, oy, f3, a, c = shared(fields, there[:6])
-            c = f3 * c
-            terms = (c * ox, c * oy, f3 * a)
-            total = plus(total, tuple(there[6] * t for t in terms))
-            back[g] = plus(back[g], tuple(mass * t for t in terms))
+            w = mass * there[6] * f3
+            c = w * c
+            terms = (c * ox, c * oy, w * a)
+            total = plus(total, terms)
+            back[g] = plus(back[g], terms)
         for k in range(3):
             sums[own[0] - 1, own[1] - 1, k] += total[k]
 
@@ -245,7 +263,6 @@
                         returned[col - 1, k, at, :] = back[g][k]
 
     def outer_row(row, step):
-        widen(row)
         outer_cell(row, 0, ((step, 1),))
         outer_cell(row, 1, ((step, 0), (step, 1)))
 
@@ -257,7 +274,6 @@
         outer_cell(row, width - 1, ((step, -1),))
 
     def inner_row(row, drs, last):
-        widen(row)
         outer_cell(row, 0, tuple((dr, 1) for dr in drs))
         outer_cell(row, width - 1, tuple((dr, -1) for dr in drs))
         down = () if last else ((1, -1), (1, 0), (1, 1))
@@ -268,20 +284,18 @@
             inner_cell(row, col, ((0, 1),) + down)
 
         inner_cell(row, width - 2, down[:2])
-        for col in range(cols - 1 if last else cols):
-            for k in range(3):
-                turned = jnp.transpose(returned[col, k])
-                total = turned[0:SUB]
-                for v in range(1, LANES // SUB):
-                    total = total + turned[v * SUB : (v + 1) * SUB]
-                sums[row - 1, col, k] += total if k == 2 else -total
+        turn(row, cols - 1 if last else cols)
 
     @pl.loop(0, cols)
     def _(col):
         for k in range(3):
             returned[col, k] = jnp.zeros((LANES, LANES), jnp.float32)
 
+    for col in range(width):
+        widen(0, col)
     outer_row(0, 1)
+    for col in range(width):
+        widen(1, col)
     inner_row(1, (0, 1), False)
 
     @pl.loop(2, height - 2)
@@ -291,16 +305,15 @@
     inner_row(height - 2, (-1, 0), True)
     outer_row(height - 1, -1)
 
-    def finish(row, peaks):
-        live = live_ref[row]
+    def finish(row, peak):
+        live = placed[row + 1, 1 : cols + 1, 7, :]
+        mass = placed[row + 1, 1 : cols + 1, 6, :]
+        per_mass = jnp.where(live > 0.0, 1.0 / mass, 0.0)
         seed = seed_ref[row]
         got = []
         for c in range(3):
-            got.append(
-                jnp.concatenate(
-                    [jnp.sum(sums[row, col, c], axis=0, keepdims=True) for col in range(cols)], axis=0
-                )
-            )
+            ends = [jnp.sum(sums[row, col, c], axis=0, keepdims=True) for col in range(cols)]
+            got.append(jnp.concatenate(ends, axis=0) * per_mass)
         acc = []
         for c in range(2):
             wind = jnp.full(seed.shape, table_ref[c, 0], jnp.float32)
@@ -309,18 +322,13 @@
             acc.append((wind - got[c]) * live)
             out_ref[c, row] = acc[c]
         out_ref[2, row] = got[2] * live
-        vx, vy = base_ref[2, row], base_ref[3, row]
-        return (
-            jnp.maximum(peaks[0], acc[0] * acc[0] + acc[1] * acc[1]),
-            jnp.maximum(peaks[1], vx * vx + vy * vy),
-        )
-
-    zero = jnp.zeros((cols, LANES), jnp.float32)
-    peaks = lax.fori_loop(0, rows, finish, (zero, zero))
-    peak_ref[...] = jnp.where(field < 4, jnp.max(peaks[0]), jnp.max(peaks[1]))
-
-
-def all_forces(counts, table, cells, seed, live, base):
+        return jnp.maximum(peak, acc[0] * acc[0] + acc[1] * acc[1])
+
+    peak = lax.fori_loop(0, rows, finish, jnp.zeros((cols, LANES), jnp.float32))
+    peak_ref[...] = jnp.full((SUB, LANES), jnp.max(peak), jnp.float32)
+
+
+def all_forces(table, cells, seed):
     height, width = cells.shape[:2]
     rows, cols = height - 2, width - 2
     which = lax.broadcasted_iota(jnp.int32, (24, FIELDS * LANES), 0) % 8
@@ -331,20 +339,21 @@
             jax.ShapeDtypeStruct((3, rows, cols, LANES), jnp.float32),
             jax.ShapeDtypeStruct((SUB, LANES), jnp.float32),
         ),
-        in_specs=[pl.BlockSpec(memory_space=pltpu.SMEM)] * 2 + [pl.BlockSpec(memory_space=pltpu.VMEM)] * 5,
+        in_specs=[pl.BlockSpec(memory_space=pltpu.SMEM)] + [pl.BlockSpec(memory_space=pltpu.VMEM)] * 3,
         out_specs=(pl.BlockSpec(memory_space=pltpu.VMEM),) * 2,
         scratch_shapes=[
             pltpu.VMEM((height, width, SUB, LANES), jnp.float32),
             pltpu.VMEM((width, LANES, FIELDS * LANES), jnp.float32),
             pltpu.VMEM((rows, cols, 3, SUB, LANES), jnp.float32),
             pltpu.VMEM((cols, 3, LANES, LANES), jnp.float32),
+            pltpu.SMEM((height, width), jnp.int32),
         ],
         compiler_params=pltpu.CompilerParams(vmem_limit_bytes=32 << 20),
-    )(counts, table, cells, pick, seed, live, base)
+    )(table, cells, pick, seed)
 
 
 def exchange_kernel(
-    groups, counts_ref, slots_ref, base_ref, moved_ref, peak_ref, got_ref, top_ref,
+    groups, counts_ref, slots_ref, base_ref, moved_ref, peak_ref, speed_ref, got_ref, top_ref,
     split, found, leaving, held, heap_a, heap_b, heap_c, send_a, recv_a, send_b, recv_b, send_c, recv_c, send_m, recv_m,
 ):
     inner, outer, near, far = groups
@@ -419,7 +428,8 @@
             device_id_type=MESH,
         )
 
-    held[0] = peak_ref[...]
+    field = lax.broadcasted_iota(jnp.int32, (SUB, LANES), 0)
+    held[0] = jnp.where(field < 4, peak_ref[...], speed_ref[...])
     stages = ((along, heap_a, send_a, recv_a), (across, heap_b, send_b, recv_b), (depth, heap_c, send_c, recv_c))
     ready = ((0, 1, 2), (3,), ())
     for step, (peers, heap, send, recv) in enumerate(stages):
@@ -466,7 +476,7 @@
             got_ref[d] = jnp.zeros(got_ref.shape[1:], jnp.float32)
 
 
-def exchange(groups, counts, slots, base, moved, peak):
+def exchange(groups, counts, slots, base, moved, peak, speed):
     inner, outer, near, far = groups
     kinds = base.shape[0] + moved.shape[0]
     cells = base.shape[1] * base.shape[2]
@@ -481,7 +491,7 @@
             jax.ShapeDtypeStruct((4, kinds, width), jnp.float32),
             jax.ShapeDtypeStruct((SUB, LANES), jnp.float32),
         ),
-        in_specs=[pl.BlockSpec(memory_space=pltpu.SMEM)] + [pl.BlockSpec(memory_space=pltpu.VMEM)] * 4,
+        in_specs=[pl.BlockSpec(memory_space=pltpu.SMEM)] + [pl.BlockSpec(memory_space=pltpu.VMEM)] * 5,
         out_specs=(pl.BlockSpec(memory_space=pltpu.VMEM),) * 2,
         scratch_shapes=[
             pltpu.VMEM((kinds * cells, 2 * LANES), jnp.bfloat16),
@@ -494,7 +504,7 @@
         ]
         + sems,
         compiler_params=pltpu.CompilerParams(collective_id=0, has_side_effects=True),
-    )(counts, slots, base, moved, peak)
+    )(counts, slots, base, moved, peak, speed)
 
 
 def advance_kernel(top_ref, base_ref, moved_ref, got_ref, state_ref, arrivals_ref):
@@ -534,12 +544,11 @@
     groups, positions, velocity, density, particle_mass, cell_count, wind_seed, wind_table, migrant_slot, migrant_count
 ):
     inner, outer, near, far = groups
-    cells, base, live = halo(
+    cells, base, speed = halo(
         inner * outer, near * far, cell_count, positions, velocity, density, particle_mass
     )
-    counts = jnp.sum(cells[:, :, 7, :], axis=2).astype(jnp.int32)
-    moved, peak = all_forces(counts, wind_table, cells, wind_seed, live, base)
-    got, top = exchange(groups, migrant_count[0, 0], migrant_slot[0, 0], base, moved, peak)
+    moved, peak = all_forces(wind_table, cells, wind_seed)
+    got, top = exchange(groups, migrant_count[0, 0], migrant_slot[0, 0], base, moved, peak, speed)
     return advance(top, base, moved, got)
 
 

time: 141 us -> 132 us (0.936)
  Pallas kernels: 132 us -> 126 us
  other arithmetic: 1.66 us -> 0.1 us
    pallas_call x1, Pallas kernels: 79 us -> 70.7 us  [all_forces(): pl.pallas_call(force_kernel, out_shape=(jax.ShapeDtypeStruct((3, rows, co...]
    pallas_call x1, Pallas kernels: 27.6 us -> 29.7 us  [exchange(): pl.pallas_call(functools.partial(exchange_kernel, groups), out_shape=(jax...]
    reduce_sum x1 -> x0, other arithmetic: 1.55 us -> none  [body(): counts = jnp.sum(cells[:, :, 7, :], axis=2).astype(jnp.int32)]
    unnamed x17 -> x13, local copies, waits for them, and re-layouts: 5.34 us -> 4.36 us
where the time goes in v3:
time: 132 us; the launch traced here: 131 us
  Pallas kernels  126 us (95%)
  local copies, waits for them, and re-layouts  4.36 us (3%)
    pallas_call x1, Pallas kernels, all_forces(): pl.pallas_call(force_kernel, out_shape=(jax.ShapeDtypeStruct((3, rows, co...  70.7 us
    pallas_call x1, Pallas kernels, exchange(): pl.pallas_call(functools.partial(exchange_kernel, groups), out_shape=(jax...  29.7 us
    pallas_call x1, Pallas kernels, halo(): pl.pallas_call(functools.partial(halo_kernel, shores, crosses), out_shape...  23.3 us
    unnamed x13, local copies, waits for them, and re-layouts  4.36 us

profile of v3, /device:TPU:1, one launch (start us, length us, event | category | flops | bytes accessed | tf_op | source)
XLA Modules:
  0.0 131.2 jit_solution(8307517664425030923)
XLA Ops:
  0.6 0.0 copy-start.5
  0.7 0.7 copy-done.5
  1.3 0.7 copy.11.count_ref
  2.0 0.1 fusion.pick_ref
  2.1 0.0 copy-start.2
  2.1 23.3 %shard_map.104 = (f32[18,10,8,128]{3,2,1,0:T(8,128)}, f32[6,16,8,128]{3,2,1,0:T(8,128)}, f32[8,128]{1,0:T(8,128)}) custom-call(s32[16,8]{1,0:T(8,128)} %copy.11.count_ref, f32[2,16,8,128]{3,2,1,0:T(8,128)} %positions_ref.1, f32[2,16,8,128]{3,2,1,0:T(8,128)} %velocity_ref.1, f32[16,8,128]{2,1,0:T(8,128)} %density_ref.1, f32[16,8,128]{2,1,0:T(8,128)} %mass_ref.1), custom_call_target="tpu_custom_call" | custom-call | tf_op jit(solution)/shard_map/pallas_call | solution.py:116
  25.4 0.0 copy-start.4
  25.4 0.0 copy-done.2
  25.4 0.7 copy-done.4
  26.1 0.0 copy-start.1
  26.1 1.1 copy-done.1
  27.2 70.7 %shard_map.105 = (f32[3,16,8,128]{3,2,1,0:T(8,128)S(1)}, f32[8,128]{1,0:T(8,128)S(1)}) custom-call(f32[2,16]{1,0:T(2,128)S(1)} %copy-done.4, f32[18,10,8,128]{3,2,1,0:T(8,128)S(1)} %copy-done.1, bf16[24,896]{1,0:T(8,128)(2,1)S(1)} %fusion.pick_ref, s32[16,8,128]{2,1,0:T(8,128)S(1)} %copy-done.2), custom_call_target="tpu_custom_call" | custom-call | tf_op jit(solution)/shard_map/pallas_call | solution.py:336
  98.0 0.0 copy-start
  98.0 0.7 copy-done
  98.6 0.0 copy-start.3
  98.6 0.6 copy-done.3
  99.2 29.7 %shard_map.106 = (f32[4,9,1792]{2,1,0:T(8,128)}, f32[8,128]{1,0:T(8,128)}) custom-call(s32[4]{0:T(128)} %bitcast.3, s32[4,1792]{1,0:T(4,128)} %bitcast.2, f32[6,16,8,128]{3,2,1,0:T(8,128)} %get-tuple-element.9.base_ref, f32[3,16,8,128]{3,2,1,0:T(8,128)} %copy-done, f32[8,128]{1,0:T(8,128)} %copy-done.3, f32[8,128]{1,0:T(8,128)} %get-tuple-element.13.speed_ref), custom_call_target="tpu_custom_call" | custom-call | tf_op jit(solution)/shard_map/pallas_call | solution.py:488
  129.0 2.3 %shard_map.107 = (f32[7,16,8,128]{3,2,1,0:T(8,128)}, f32[1,1,4,8,1792]{4,3,2,1,0:T(8,128)}) custom-call(f32[8,128]{1,0:T(8,128)} %get-tuple-element.14.top_ref, f32[6,16,8,128]{3,2,1,0:T(8,128)} %get-tuple-element.9.base_ref, f32[3,16,8,128]{3,2,1,0:T(8,128)} %copy-done, f32[4,9,1792]{2,1,0:T(8,128)} %get-tuple-element.15.got_ref), custom_call_target="tpu_custom_call" | custom-call | tf_op jit(solution)/shard_map/pallas_call | solution.py:532
  (4 shorter events, 0.0 us)
Async XLA Ops:
  0.6 0.7 copy-start.5
  2.1 23.3 %copy-start.2 = (s32[16,8,128]{2,1,0:T(8,128)S(1)}, s32[16,8,128]{2,1,0:T(8,128)}, u32[]{:S(2)}) copy-start(s32[16,8,128]{2,1,0:T(8,128)} %seed_ref.1) | copy-start | bytes 196612
  25.4 0.7 copy-start.4
  26.1 1.1 copy-start.1
  98.0 0.7 copy-start
  98.6 0.6 copy-start.3

commit v4 on v3

--- a/solution.py
+++ b/solution.py
@@ -43,9 +43,9 @@
     slot = lax.broadcasted_iota(jnp.int32, (cols, LANES), 1)
 
     def pack(row, fastest):
-        filled = jnp.full((cols, LANES), count_ref[row, 0], jnp.int32)
+        filled = jnp.full((cols, LANES), count_ref[0, row], jnp.int32)
         for col in range(1, cols):
-            filled = jnp.where(which == col, count_ref[row, col], filled)
+            filled = jnp.where(which == col, count_ref[col, row], filled)
         live = jnp.where(slot < filled, 1.0, 0.0)
         x, y, u, v = positions_ref[0, row], positions_ref[1, row], velocity_ref[0, row], velocity_ref[1, row]
         dense = density_ref[row]
@@ -172,12 +172,6 @@
                 total = total + turned[v * SUB : (v + 1) * SUB]
             sums[row - 1, col, k] += total if k == 2 else -total
 
-    def turn(row, gathered):
-        for col in range(width):
-            widen(row + 1, col)
-            if col < gathered:
-                gather_back(row, col)
-
     def loop_over(row, col):
         count = lax.div(counts[row, col] + (SUB * GROUP - 1), SUB * GROUP)
 
@@ -222,7 +216,7 @@
         for k in range(3):
             sums[own[0] - 1, own[1] - 1, k] += total[k]
 
-    def both_ways(row, col, step, near, back):
+    def both_ways(row, col, step, near, back, keep):
         own = (row + step[0], col + step[1])
         fields = [row_of(own[0], own[1], f) for f in range(6)]
         mass = row_of(own[0], own[1], 6)
@@ -234,19 +228,11 @@
             terms = (c * ox, c * oy, w * a)
             total = plus(total, terms)
             back[g] = plus(back[g], terms)
-        for k in range(3):
-            sums[own[0] - 1, own[1] - 1, k] += total[k]
-
-    def outer_cell(row, col, steps):
-        count, loaded = loop_over(row, col)
-
-        @pl.loop(0, count)
-        def _(part):
-            near = loaded(part)
-            for step in steps:
-                one_way(row, col, step, near)
-
-    def inner_cell(row, col, steps):
+        if keep:
+            for k in range(3):
+                sums[own[0] - 1, own[1] - 1, k] += total[k]
+
+    def one_cell(row, col, mutual, rim):
         count, loaded = loop_over(row, col)
 
         @pl.loop(0, count)
@@ -254,56 +240,53 @@
             near = loaded(part)
             back = [None] * GROUP
             one_way(row, col, (0, 0), near)
-            for step in steps:
-                both_ways(row, col, step, near, back)
+            for step in mutual:
+                both_ways(row, col, step, near, back, True)
+            for step in rim:
+                both_ways(row, col, step, near, back, False)
             for g in range(GROUP):
-                if back[g] is not None:
-                    at = pl.ds(pl.multiple_of((part * GROUP + g) * SUB, SUB), SUB)
-                    for k in range(3):
-                        returned[col - 1, k, at, :] = back[g][k]
-
-    def outer_row(row, step):
-        outer_cell(row, 0, ((step, 1),))
-        outer_cell(row, 1, ((step, 0), (step, 1)))
-
-        @pl.loop(2, width - 2)
+                at = pl.ds(pl.multiple_of((part * GROUP + g) * SUB, SUB), SUB)
+                for k in range(3):
+                    returned[col - 1, k, at, :] = back[g][k]
+
+    def one_row(row, first, last):
+        def cell(col, leftmost, rightmost):
+            mutual, rim = [], []
+            for step in ((-1, -1), (-1, 0), (-1, 1), (0, -1), (0, 1), (1, -1), (1, 0), (1, 1)):
+                dr, dc = step
+                outside = (first and dr < 0) or (last and dr > 0) or (leftmost and dc < 0) or (rightmost and dc > 0)
+                if outside:
+                    rim.append(step)
+                elif dr > 0 or (dr == 0 and dc > 0):
+                    mutual.append(step)
+            one_cell(row, col, mutual, rim)
+
+        cell(1, True, False)
+
+        @pl.loop(2, cols)
         def _(col):
-            outer_cell(row, col, ((step, -1), (step, 0), (step, 1)))
-
-        outer_cell(row, width - 2, ((step, -1), (step, 0)))
-        outer_cell(row, width - 1, ((step, -1),))
-
-    def inner_row(row, drs, last):
-        outer_cell(row, 0, tuple((dr, 1) for dr in drs))
-        outer_cell(row, width - 1, tuple((dr, -1) for dr in drs))
-        down = () if last else ((1, -1), (1, 0), (1, 1))
-        inner_cell(row, 1, ((0, 1),) + down[1:])
-
-        @pl.loop(2, width - 2)
-        def _(col):
-            inner_cell(row, col, ((0, 1),) + down)
-
-        inner_cell(row, width - 2, down[:2])
-        turn(row, cols - 1 if last else cols)
+            cell(col, False, False)
+
+        cell(cols, False, True)
+        for col in range(1, cols + 1):
+            if not last:
+                widen(row + 1, col)
+            gather_back(row, col - 1)
 
     @pl.loop(0, cols)
     def _(col):
         for k in range(3):
             returned[col, k] = jnp.zeros((LANES, LANES), jnp.float32)
 
-    for col in range(width):
-        widen(0, col)
-    outer_row(0, 1)
-    for col in range(width):
+    for col in range(1, cols + 1):
         widen(1, col)
-    inner_row(1, (0, 1), False)
-
-    @pl.loop(2, height - 2)
+    one_row(1, True, False)
+
+    @pl.loop(2, rows)
     def _(row):
-        inner_row(row, (-1, 0, 1), False)
-
-    inner_row(height - 2, (-1, 0), True)
-    outer_row(height - 1, -1)
+        one_row(row, False, False)
+
+    one_row(rows, False, True)
 
     def finish(row, peak):
         live = placed[row + 1, 1 : cols + 1, 7, :]
@@ -416,6 +399,7 @@
 
     gather(0)
     gather(1)
+    gather(2)
     pl.semaphore_wait(barrier, len(greeted))
 
     def migrants(d):
@@ -431,7 +415,7 @@
     field = lax.broadcasted_iota(jnp.int32, (SUB, LANES), 0)
     held[0] = jnp.where(field < 4, peak_ref[...], speed_ref[...])
     stages = ((along, heap_a, send_a, recv_a), (across, heap_b, send_b, recv_b), (depth, heap_c, send_c, recv_c))
-    ready = ((0, 1, 2), (3,), ())
+    ready = ((0, 1, 2, 3), (), ())
     for step, (peers, heap, send, recv) in enumerate(stages):
         copies = [
             pltpu.make_async_remote_copy(
@@ -447,7 +431,7 @@
         for copy in copies:
             copy.start()
         for d in ready[step]:
-            if d > 1:
+            if d > 2:
                 gather(d)
 
             @pl.when(ends[d][0])
@@ -545,7 +529,7 @@
 ):
     inner, outer, near, far = groups
     cells, base, speed = halo(
-        inner * outer, near * far, cell_count, positions, velocity, density, particle_mass
+        inner * outer, near * far, cell_count.T, positions, velocity, density, particle_mass
     )
     moved, peak = all_forces(wind_table, cells, wind_seed)
     got, top = exchange(groups, migrant_count[0, 0], migrant_slot[0, 0], base, moved, peak, speed)

time: 132 us -> 128 us (0.970)
  Pallas kernels: 126 us -> 123 us
  local copies, waits for them, and re-layouts: 4.36 us -> 3.04 us
    pallas_call x1, Pallas kernels: 29.7 us -> 27.9 us  [exchange(): pl.pallas_call(functools.partial(exchange_kernel, groups), out_shape=(jax...]
    unnamed x13 -> x10, local copies, waits for them, and re-layouts: 4.36 us -> 3.04 us
where the time goes in v4:
time: 128 us; the launch traced here: 127 us
  Pallas kernels  123 us (96%)
  local copies, waits for them, and re-layouts  3.04 us (2%)
    pallas_call x1, Pallas kernels, all_forces(): pl.pallas_call(force_kernel, out_shape=(jax.ShapeDtypeStruct((3, rows, co...  69.7 us
    pallas_call x1, Pallas kernels, exchange(): pl.pallas_call(functools.partial(exchange_kernel, groups), out_shape=(jax...  27.9 us
    pallas_call x1, Pallas kernels, halo(): pl.pallas_call(functools.partial(halo_kernel, shores, crosses), out_shape...  23.3 us
    unnamed x10, local copies, waits for them, and re-layouts  3.04 us

profile of v4, /device:TPU:1, one launch (start us, length us, event | category | flops | bytes accessed | tf_op | source)
XLA Modules:
  0.0 127.0 jit_solution(12182691841632675118)
XLA Ops:
  0.7 0.1 fusion.pick_ref
  0.8 0.0 copy-start.2
  0.8 23.3 %shard_map.104 = (f32[18,10,8,128]{3,2,1,0:T(8,128)}, f32[6,16,8,128]{3,2,1,0:T(8,128)}, f32[8,128]{1,0:T(8,128)}) custom-call(s32[8,16]{1,0:T(8,128)} %bitcast.4, f32[2,16,8,128]{3,2,1,0:T(8,128)} %positions_ref.1, f32[2,16,8,128]{3,2,1,0:T(8,128)} %velocity_ref.1, f32[16,8,128]{2,1,0:T(8,128)} %density_ref.1, f32[16,8,128]{2,1,0:T(8,128)} %mass_ref.1), custom_call_target="tpu_custom_call" | custom-call | tf_op jit(solution)/shard_map/pallas_call | solution.py:116
  24.1 0.0 copy-start.4
  24.1 0.0 copy-done.2
  24.1 0.7 copy-done.4
  24.8 0.0 copy-start.1
  24.8 1.1 copy-done.1
  25.9 69.7 %shard_map.105 = (f32[3,16,8,128]{3,2,1,0:T(8,128)S(1)}, f32[8,128]{1,0:T(8,128)S(1)}) custom-call(f32[2,16]{1,0:T(2,128)S(1)} %copy-done.4, f32[18,10,8,128]{3,2,1,0:T(8,128)S(1)} %copy-done.1, bf16[24,896]{1,0:T(8,128)(2,1)S(1)} %fusion.pick_ref, s32[16,8,128]{2,1,0:T(8,128)S(1)} %copy-done.2), custom_call_target="tpu_custom_call" | custom-call | tf_op jit(solution)/shard_map/pallas_call | solution.py:319
  95.6 0.0 copy-start
  95.6 0.7 copy-done
  96.3 0.0 copy-start.3
  96.3 0.6 copy-done.3
  96.9 27.9 %shard_map.106 = (f32[4,9,1792]{2,1,0:T(8,128)}, f32[8,128]{1,0:T(8,128)}) custom-call(s32[4]{0:T(128)} %bitcast.5, s32[4,1792]{1,0:T(4,128)} %bitcast.3, f32[6,16,8,128]{3,2,1,0:T(8,128)} %get-tuple-element.9.base_ref, f32[3,16,8,128]{3,2,1,0:T(8,128)} %copy-done, f32[8,128]{1,0:T(8,128)} %copy-done.3, f32[8,128]{1,0:T(8,128)} %get-tuple-element.13.speed_ref), custom_call_target="tpu_custom_call" | custom-call | tf_op jit(solution)/shard_map/pallas_call | solution.py:472
  124.8 2.3 %shard_map.107 = (f32[7,16,8,128]{3,2,1,0:T(8,128)}, f32[1,1,4,8,1792]{4,3,2,1,0:T(8,128)}) custom-call(f32[8,128]{1,0:T(8,128)} %get-tuple-element.14.top_ref, f32[6,16,8,128]{3,2,1,0:T(8,128)} %get-tuple-element.9.base_ref, f32[3,16,8,128]{3,2,1,0:T(8,128)} %copy-done, f32[4,9,1792]{2,1,0:T(8,128)} %get-tuple-element.15.got_ref), custom_call_target="tpu_custom_call" | custom-call | tf_op jit(solution)/shard_map/pallas_call | solution.py:516
  (4 shorter events, 0.0 us)
Async XLA Ops:
  0.8 23.4 %copy-start.2 = (s32[16,8,128]{2,1,0:T(8,128)S(1)}, s32[16,8,128]{2,1,0:T(8,128)}, u32[]{:S(2)}) copy-start(s32[16,8,128]{2,1,0:T(8,128)} %seed_ref.1) | copy-start | bytes 196612
  24.1 0.7 copy-start.4
  24.8 1.1 copy-start.1
  95.6 0.7 copy-start
  96.3 0.6 copy-start.3
